TPU v7x, 128 devices: a whole 4x4x4 slice. The times are simulated.
128 devices in a mesh: wide: 8 (over z, x_hi), narrow: 4 (over y), depth: 4 (over x_lo, core).
Axes of the slice: x: 4 (x_hi: 2, x_lo: 2; x = x_hi * 2 + x_lo), y: 4, z: 4, core: 2. Of those that a mesh axis runs over, the one named last changes fastest.
Arguments:
- hidden_in: bfloat16 [2048, 4096], P(('wide', 'narrow'), 'depth'), may hold values from -36 to 36
- queries: bfloat16 [2048, 4096], P('wide', ('narrow', 'depth')), may hold values from -8 to 8
- lang_ids: int32 [2048], replicated, may hold values from 0 to 7
- owner_slot: int32 [8], replicated, may hold values from 0 to 7, each once
- enc_kv: bfloat16 [8, 2, 768, 4096], P('wide', None, None, ('narrow', 'depth')), may hold values from -7 to 7
- attn_proj: bfloat16 [4096, 4096], P(('narrow', 'depth')), may hold values from -0.09375 to 0.09375
- norm_gain: float32 [4096], replicated, may hold values from 0.25 to 1.75
- router_proj: float32 [4096, 4], replicated, may hold values from -0.09375 to 0.09375
- expert_ids: int32 [2048, 2], P('wide'), may hold values from 0 to 3, all different within a row; in each aligned block of 64 rows (0 to 63, 64 to 127, ...) at most 48 rows name the same one
- proj_in: bfloat16 [4, 4096, 5120], P('narrow', None, 'depth'), may hold values from -0.09375 to 0.09375
- proj_out: bfloat16 [4, 5120, 4096], P('narrow', 'depth'), may hold values from -0.078125 to 0.078125
Outputs:
- layer_out: bfloat16 [2048, 4096], P(('wide', 'narrow'), 'depth')
Inputs may be any that keep to these rules, and one draw needn't show every extreme that they name: `owner_slot`: every slot once. `expert_ids`: each row names two different experts. Within each aligned block of 64 rows (the rows of one index of wide+narrow) no expert is named more than 48 times, a bound that some block reaches.
All inputs are finite; a program needn't handle non-finite values.
Results may differ from a plain program's by a relative error of at most 0.017.
Values may be sent and summed in bfloat16 or wider, within the bound.
A program may use at most 128 MiB of HBM per device.

v0:
```python
import math

import jax
import jax.numpy as jnp
from jax import lax
from jax.sharding import PartitionSpec as P

HEAD_DIM = 64
CAP = 48


neg_big = -1e30
norm_eps = 1e-06


def in_order(blocks, dim):
    shape = list(blocks.shape[1:])
    shape[dim] *= blocks.shape[0]
    return jnp.moveaxis(blocks, 0, dim).reshape(shape)


def sent_to_all(value, axis):
    peers = lax.axis_size(axis)
    return lax.all_to_all(
        jnp.broadcast_to(value[None], (peers, *value.shape)), axis, 0, 0, tiled=True
    )


def collect(value, axis, dim):
    return in_order(sent_to_all(value, axis), dim)


def in_blocks(value, dim, peers):
    before, after = (value.shape[:dim], value.shape[dim + 1 :])
    return jnp.moveaxis(value.reshape(*before, peers, -1, *after), dim, 0)


def sum_at_owner(value, axis, dim):
    blocks = in_blocks(value, dim, lax.axis_size(axis))
    arrived = lax.all_to_all(blocks, axis, split_axis=0, concat_axis=0, tiled=True)
    return arrived.astype(jnp.float32).sum(axis=0)


def empty_state(row_count, head_count):
    return (
        jnp.full((row_count, head_count), neg_big, jnp.float32),
        jnp.zeros((row_count, head_count), jnp.float32),
        jnp.zeros((row_count, head_count, HEAD_DIM), jnp.float32),
    )


def slot_update(running, query_rows, key_rows, value_rows, is_live):
    run_max, run_sum, run_acc = running
    scores = jnp.einsum(
        "rhd,khd->rhk", query_rows, key_rows, preferred_element_type=jnp.float32
    ) * HEAD_DIM ** (-0.5)
    new_max = jnp.where(is_live[:, None], jnp.maximum(run_max, jnp.max(scores, axis=2)), run_max)
    weights = jnp.where(is_live[:, None, None], jnp.exp(scores - new_max[:, :, None]), 0.0)
    shrink = jnp.exp(run_max - new_max)
    run_sum = run_sum * shrink + jnp.sum(weights, axis=2)
    taken_sum = jnp.einsum(
        "rhk,khd->rhd", weights.astype(jnp.bfloat16), value_rows, preferred_element_type=jnp.float32
    )
    return (new_max, run_sum, run_acc * shrink[:, :, None] + taken_sum)


def slot_scan(running, kv_block, first_slot, query_rows, slot_tags):
    head_count = query_rows.shape[1]

    def visit_slot(carried, element):
        kv_pair, position = element
        key_rows = kv_pair[0].reshape(kv_pair.shape[1], head_count, HEAD_DIM)
        value_rows = kv_pair[1].reshape(kv_pair.shape[1], head_count, HEAD_DIM)
        return (slot_update(carried, query_rows, key_rows, value_rows, slot_tags == position), None)

    positions = first_slot + jnp.arange(kv_block.shape[0], dtype=jnp.int32)
    running, _ = lax.scan(visit_slot, running, (kv_block, positions))
    return running


def finish(running):
    run_max, run_sum, run_acc = running
    safe_sum = jnp.where(run_sum > 0.0, run_sum, 1.0)
    return (run_acc / safe_sum[:, :, None]).reshape(run_acc.shape[0], -1)


def assign_slots(choice_ids, experts):
    pick_flags = (
        choice_ids[:, :, None] == jnp.arange(experts, dtype=jnp.int32)[None, None, :]
    ).astype(jnp.int32)
    flat_flags = pick_flags.reshape(-1, experts)
    before = jnp.cumsum(flat_flags, axis=0) - flat_flags
    slot_rank = jnp.sum(before * flat_flags, axis=1).reshape(choice_ids.shape)
    return choice_ids * CAP + slot_rank


def make_worker(proj_in, proj_out, depth_count, quarter):
    experts_here = proj_in.shape[0]
    out_blocks = proj_out.reshape(experts_here, proj_out.shape[1], depth_count, quarter)

    def expert_ffn(arrived):
        sources = arrived.shape[0] // experts_here
        slot_count = arrived.shape[1]
        grid_rows = arrived.reshape(sources, experts_here, slot_count, arrived.shape[2])
        hidden_act = jnp.einsum(
            "secd,edf->secf", grid_rows, proj_in, preferred_element_type=jnp.float32
        )
        hidden_act = jax.nn.gelu(hidden_act, approximate=True).astype(jnp.bfloat16)
        expert_part = jnp.einsum(
            "secf,efgq->gsecq", hidden_act, out_blocks, preferred_element_type=jnp.float32
        )
        expert_part = expert_part.reshape(depth_count, sources * experts_here, slot_count, quarter)
        return expert_part

    return expert_ffn


def shards(
    hidden_in,
    queries,
    lang_ids,
    owner_slot,
    enc_kv,
    attn_proj,
    norm_gain,
    router_proj,
    expert_ids,
    proj_in,
    proj_out,
):
    narrow_count = lax.axis_size("narrow")
    depth_count = lax.axis_size("depth")
    tok_rows = hidden_in.shape[0]
    quarter = hidden_in.shape[1]
    head_count = queries.shape[1] // HEAD_DIM
    lang_count = owner_slot.shape[0]
    experts_here = proj_in.shape[0]
    experts = experts_here * narrow_count
    lang_match = lang_ids[:, None] == jnp.arange(lang_count, dtype=jnp.int32)[None, :]
    holder = jnp.sum(jnp.where(lang_match, owner_slot[None, :], 0), axis=1)
    first_slot = lax.axis_index("wide") * enc_kv.shape[0]
    segment = collect(queries, "wide", 0)
    row_count = segment.shape[0]
    block_rows = math.gcd(row_count, 512)

    def one_block(element):
        part_rows, part_tags = element
        running = slot_scan(
            empty_state(block_rows, head_count),
            enc_kv,
            first_slot,
            part_rows.reshape(block_rows, head_count, HEAD_DIM),
            part_tags,
        )
        return finish(running)

    blocks_out = lax.map(
        one_block,
        (
            segment.reshape(row_count // block_rows, block_rows, segment.shape[1]),
            holder.reshape(row_count // block_rows, block_rows),
        ),
    )
    partial_context = blocks_out.reshape(row_count, segment.shape[1])
    context = sum_at_owner(partial_context.astype(jnp.bfloat16), "wide", 0).astype(jnp.bfloat16)
    context_blocks = context.reshape(narrow_count, tok_rows, context.shape[1])
    proj_blocks = attn_proj.reshape(attn_proj.shape[0], depth_count, quarter)

    def pair_term(pair_index):
        row_block = lax.dynamic_index_in_dim(
            context_blocks, pair_index // depth_count, 0, keepdims=False
        )
        col_block = lax.dynamic_index_in_dim(
            proj_blocks, pair_index % depth_count, 1, keepdims=False
        )
        return jnp.dot(row_block, col_block, preferred_element_type=jnp.float32)

    pair_ids = jnp.arange(
        tok_rows * lax.axis_size(("narrow", "depth")) // tok_rows, dtype=jnp.int32
    )
    attn_out = sum_at_owner(
        lax.map(pair_term, pair_ids)
        .reshape(tok_rows * lax.axis_size(("narrow", "depth")), quarter)
        .astype(jnp.bfloat16),
        ("narrow", "depth"),
        0,
    )
    residual = (hidden_in.astype(jnp.float32) + attn_out).astype(jnp.bfloat16)
    full_rows = lax.all_gather(residual, "depth", axis=1, tiled=True).astype(jnp.float32)
    inv_norm = lax.rsqrt(jnp.mean(full_rows * full_rows, axis=1) + norm_eps)
    normed = (full_rows * inv_norm[:, None] * norm_gain[None, :]).astype(jnp.bfloat16)
    narrow_at = lax.axis_index("narrow")
    own_ids = lax.dynamic_slice_in_dim(expert_ids, narrow_at * tok_rows, tok_rows, 0)
    targets = assign_slots(own_ids, experts)
    lane_ids = jnp.arange(experts * CAP, dtype=jnp.int32)
    dispatch_mask = jnp.any(lane_ids[:, None, None] == targets[None, :, :], axis=2).astype(
        jnp.bfloat16
    )
    outbox = jnp.dot(dispatch_mask, normed, preferred_element_type=jnp.float32).astype(jnp.bfloat16)
    outbox = outbox.reshape(experts, CAP, normed.shape[1])
    worker = make_worker(proj_in, proj_out, depth_count, quarter)
    arrived_out = worker(lax.all_to_all(outbox, "narrow", split_axis=0, concat_axis=0, tiled=True))
    summed = sum_at_owner(arrived_out.astype(jnp.bfloat16), "depth", 0)
    returned = lax.all_to_all(
        summed.astype(jnp.bfloat16), "narrow", split_axis=1, concat_axis=1, tiled=True
    ).astype(summed.dtype)
    logits = jnp.dot(normed.astype(jnp.float32), router_proj, precision=lax.Precision.HIGHEST)
    pick_mask = own_ids[:, :, None] == jnp.arange(experts, dtype=jnp.int32)[None, None, :]
    own_logit = jnp.sum(jnp.where(pick_mask, logits[:, None, :], 0.0), axis=2)
    gates = jax.nn.sigmoid(own_logit - own_logit[:, ::-1])
    picked = jnp.take(
        returned.reshape(experts * CAP, quarter), targets.reshape(-1), axis=0
    ).reshape(tok_rows, 2, quarter)
    combined = jnp.sum(gates[:, :, None] * picked, axis=1)
    return (residual.astype(jnp.float32) + combined).astype(jnp.bfloat16)


def solution(mesh):
    return jax.shard_map(
        shards,
        mesh=mesh,
        in_specs=(
            P(("wide", "narrow"), "depth"),
            P("wide", ("narrow", "depth")),
            P(),
            P(),
            P("wide", None, None, ("narrow", "depth")),
            P(("narrow", "depth"), None),
            P(),
            P(),
            P("wide", None),
            P("narrow", None, "depth"),
            P("narrow", "depth", None),
        ),
        out_specs=P(("wide", "narrow"), "depth"),
        check_vma=False,
    )
```

profile of v0, /device:TPU:0, one launch (start us, length us, event | category | flops | bytes accessed | tf_op | source)
XLA Modules:
  0.0 258.0 jit_solution(7034597366299841906)
XLA Ops:
  0.0 2.0 broadcast_in_dim.114
  2.0 7.9 %all-to-all-start = ((bf16[8,256,256]{2,1,0:T(8,128)(2,1)}), bf16[8,256,256]{2,1,0:T(8,128)(2,1)S(1)}, u32[]{:S(2)}, u32[]{:S(2)}) async-start(bf16[8,256,256]{2,1,0:T(8,128)(2,1)} %broadcast_in_dim.114), calls=%async_computation | async-start | bytes 2097152 | tf_op jit(solution)/shard_map/all_to_all | solution.py:24
  12.1 15.0 %all-to-all-done = bf16[8,256,256]{2,1,0:T(8,128)(2,1)S(1)} async-done(((bf16[8,256,256]{2,1,0:T(8,128)(2,1)}), bf16[8,256,256]{2,1,0:T(8,128)(2,1)S(1)}, u32[]{:S(2)}, u32[]{:S(2)}) %all-to-all-start) | async-done | bytes 1048608 | tf_op jit(solution)/shard_map/all_to_all | solution.py:24
  27.1 20.3 %while.28 = (s32[]{:T(128)}, bf16[4,512,256]{2,1,0:T(8,128)(2,1)S(1)}, s32[4,512]{1,0:T(4,128)S(1)}, s32[]{:T(128)}, bf16[4,512,256]{2,1,0:T(8,128)(2,1)S(1)}, /*index=5*/bf16[1,2,768,256]{2,3,1,0:T(8,128)(2,1)S(1)}, s32[]{:T(128)}) while((s32[]{:T(128)}, bf16[4,512,256]{2,1,0:T(8,128)(2,1)S(1)}, s32[4,512]{1,0:T(4,128)S(1)}, s32[]{:T(128)}, ...), condition=%wide.region_4.5_spmd, body=%wide.region_1.4_spmd.sunk | while | flops 418789888 | bytes 23957604 | solution.py:157
  30.2 1.8 fusion.95
  35.3 1.8 fusion.95
  40.3 1.8 fusion.95
  48.4 3.6 %all-to-all-start.1 = ((bf16[8,256,256]{2,1,0:T(8,128)(2,1)}), bf16[8,256,256]{2,1,0:T(8,128)(2,1)S(1)}, u32[]{:S(2)}, u32[]{:S(2)}) async-start(bf16[8,256,256]{2,1,0:T(8,128)(2,1)} %bitcast.143), calls=%async_computation.1 | async-start | bytes 2097152 | tf_op jit(solution)/shard_map/all_to_all | solution.py:40
  51.9 3.3 %copy.53 = bf16[256,4096]{0,1:T(8,128)(2,1)S(1)} copy(bf16[256,4096]{1,0:T(8,128)(2,1)} %param.20) | data formatting | bytes 4194304 | tf_op args[5]
  55.2 13.2 %all-to-all-done.1 = bf16[8,256,256]{2,1,0:T(8,128)(2,1)S(1)} async-done(((bf16[8,256,256]{2,1,0:T(8,128)(2,1)}), bf16[8,256,256]{2,1,0:T(8,128)(2,1)S(1)}, u32[]{:S(2)}, u32[]{:S(2)}) %all-to-all-start.1) | async-done | bytes 1048608 | tf_op jit(solution)/shard_map/all_to_all | solution.py:40
  68.6 64.6 %while.29 = (s32[]{:T(128)}, bf16[16,64,1024]{2,1,0:T(8,128)(2,1)}, s32[16]{0:T(128)S(1)}, bf16[4,64,256]{2,1,0:T(8,128)(2,1)S(1)}, bf16[256,4,1024]{0,2,1:T(8,1...) while((s32[]{:T(128)}, bf16[16,64,1024]{2,1,0:T(8,128)(2,1)}, ...), condition=%wide.region_7.8_spmd, body=%wide.region_6.7_spmd.sunk | while | flops 33554456 | bytes 819596 | solution.py:182
  133.3 4.6 %all-to-all-start.2 = ((bf16[16,64,1024]{2,1,0:T(8,128)(2,1)}), bf16[16,64,1024]{2,1,0:T(8,128)(2,1)S(1)}, u32[]{:S(2)}, u32[]{:S(2)}) async-start(bf16[16,64,1024]{2,1,0:T(8,128)(2,1)} %get-tuple-element.130), calls=%async_computation.2 | async-start | bytes 4194304 | tf_op jit(solution)/shard_map/all_to_all | solution.py:40
  139.1 26.6 %all-to-all-done.2 = bf16[16,64,1024]{2,1,0:T(8,128)(2,1)S(1)} async-done(((bf16[16,64,1024]{2,1,0:T(8,128)(2,1)}), bf16[16,64,1024]{2,1,0:T(8,128)(2,1)S(1)}, u32[]{:S(2)}, u32[]{:S(2)}) %all-to-all-start.2) | async-done | bytes 2097184 | tf_op jit(solution)/shard_map/all_to_all | solution.py:40
  166.1 6.5 %all_gather.3 = bf16[64,4096]{1,0:T(8,128)(2,1)S(1)} all-gather(bf16[64,1024]{1,0:T(8,128)(2,1)S(1)} %add_convert_fusion.1), channel_id=1, replica_groups=mesh['wide'=8,'narrow'=4,'depth'=4] {'depth'}, dimensions={1}, use_global_device_ids=true | all-gather | bytes 655360 | tf_op jit(solution)/shard_map/all_gather | solution.py:189
  172.8 1.8 convolution_convert_fusion
  174.6 3.7 %all-to-all-start.3 = ((bf16[4,48,4096]{2,1,0:T(8,128)(2,1)}), bf16[4,48,4096]{2,1,0:T(8,128)(2,1)S(1)}, u32[]{:S(2)}, u32[]{:S(2)}) async-start(bf16[4,48,4096]{2,1,0:T(8,128)(2,1)} %bitcast.14), calls=%async_computation.3 | async-start | bytes 3145728 | tf_op jit(solution)/shard_map/all_to_all | solution.py:202
  178.4 17.8 %reshape.205 = bf16[1280,4,1024]{2,1,0:T(4,128)(2,1)} reshape(bf16[1,1280,4096]{2,1,0:T(8,128)(2,1)} %param.25) | data formatting | bytes 20971520 | tf_op jit(solution)/shard_map/reshape.14
  196.2 3.5 %all-to-all-done.3 = bf16[4,48,4096]{2,1,0:T(8,128)(2,1)S(1)} async-done(((bf16[4,48,4096]{2,1,0:T(8,128)(2,1)}), bf16[4,48,4096]{2,1,0:T(8,128)(2,1)S(1)}, u32[]{:S(2)}, u32[]{:S(2)}) %all-to-all-start.3) | async-done | bytes 1572896 | tf_op jit(solution)/shard_map/all_to_all | solution.py:202
  199.7 16.7 %fusion.35 = bf16[4,1,4,48,1024]{4,3,0,2,1:T(8,128)(2,1)} fusion(bf16[1280,4,1024]{2,1,0:T(4,128)(2,1)} %reshape.205, bf16[4,48,4096]{2,1,0:T(8,128)(2,1)S(1)} %all-to-all-done.3, bf16[1,4096,1280]{2,1,0:T(8,128)(2,1)} %param.24), kind=kOutput, calls=%fused_computation.36 | convolution fusion | flops 4029530112 | bytes 24117248 | tf_op jit(solution)/shard_map/secf,efgq->gsecq/dot_general | solution.py:109
  216.4 2.7 %copy.60 = bf16[4,1,4,48,1024]{4,3,2,1,0:T(8,128)(2,1)} copy(bf16[4,1,4,48,1024]{4,3,0,2,1:T(8,128)(2,1)} %fusion.35) | data formatting | bytes 3145728 | tf_op jit(solution)/shard_map/convert_element_type | solution.py:203
  219.1 3.6 %all-to-all-start.4 = ((bf16[4,1,4,48,1024]{4,3,2,1,0:T(8,128)(2,1)}), bf16[4,1,4,48,1024]{4,3,2,1,0:T(8,128)(2,1)S(1)}, u32[]{:S(2)}, u32[]{:S(2)}) async-start(bf16[4,1,4,48,1024]{4,3,2,1,0:T(8,128)(2,1)} %copy.60), calls=%async_computation.4 | async-start | bytes 3145728 | tf_op jit(solution)/shard_map/all_to_all | solution.py:40
  223.6 19.0 %all-to-all-done.4 = bf16[4,1,4,48,1024]{4,3,2,1,0:T(8,128)(2,1)S(1)} async-done(((bf16[4,1,4,48,1024]{4,3,2,1,0:T(8,128)(2,1)}), bf16[4,1,4,48,1024]{4,3,2,1,0:T(8,128)(2,1)S(1)}, u32[]{:S(2)}, u32[]{:S(2)}) %all-to-all-start.4) | async-done | bytes 1572896 | tf_op jit(solution)/shard_map/all_to_all | solution.py:40
  243.8 3.5 %all-to-all-start.5 = ((bf16[1,4,48,1024]{3,2,0,1:T(8,128)(2,1)}), bf16[1,4,48,1024]{3,2,0,1:T(8,128)(2,1)S(1)}, u32[]{:S(2)}, u32[]{:S(2)}) async-start(bf16[1,4,48,1024]{3,2,0,1:T(8,128)(2,1)} %bitcast.30), calls=%async_computation.5 | async-start | bytes 786432 | tf_op jit(solution)/shard_map/all_to_all | solution.py:204
  247.4 7.9 %all-to-all-done.5 = bf16[1,4,48,1024]{3,2,0,1:T(8,128)(2,1)S(1)} async-done(((bf16[1,4,48,1024]{3,2,0,1:T(8,128)(2,1)}), bf16[1,4,48,1024]{3,2,0,1:T(8,128)(2,1)S(1)}, u32[]{:S(2)}, u32[]{:S(2)}) %all-to-all-start.5) | async-done | bytes 393248 | tf_op jit(solution)/shard_map/all_to_all | solution.py:204
  (120 shorter events, 49.3 us)
Async XLA Ops:
  0.0 223.0 %copy-start = (f32[4096,4]{0,1:T(4,128)S(1)}, f32[4096,4]{0,1:T(4,128)}, u32[]{:S(2)}) copy-start(f32[4096,4]{0,1:T(4,128)} %param.22) | copy-start | bytes 196612
  2.0 25.1 %all-to-all-start = ((bf16[8,256,256]{2,1,0:T(8,128)(2,1)}), bf16[8,256,256]{2,1,0:T(8,128)(2,1)S(1)}, u32[]{:S(2)}, u32[]{:S(2)}) async-start(bf16[8,256,256]{2,1,0:T(8,128)(2,1)} %broadcast_in_dim.114), calls=%async_computation | async-start | bytes 2097152 | tf_op jit(solution)/shard_map/all_to_all | solution.py:24
  47.4 1.0 copy-start.1
  48.4 20.1 %all-to-all-start.1 = ((bf16[8,256,256]{2,1,0:T(8,128)(2,1)}), bf16[8,256,256]{2,1,0:T(8,128)(2,1)S(1)}, u32[]{:S(2)}, u32[]{:S(2)}) async-start(bf16[8,256,256]{2,1,0:T(8,128)(2,1)} %bitcast.143), calls=%async_computation.1 | async-start | bytes 2097152 | tf_op jit(solution)/shard_map/all_to_all | solution.py:40
  51.9 85.9 %copy-start.4 = (s32[256,2]{0,1:T(2,128)S(1)}, s32[256,2]{0,1:T(2,128)}, u32[]{:S(2)}) copy-start(s32[256,2]{0,1:T(2,128)} %param.23) | copy-start | bytes 6148
  55.2 110.8 %copy-start.2 = (bf16[64,1024]{1,0:T(8,128)(2,1)S(1)}, bf16[64,1024]{1,0:T(8,128)(2,1)}, u32[]{:S(2)}) copy-start(bf16[64,1024]{1,0:T(8,128)(2,1)} %param.15) | copy-start | bytes 393220
  68.6 104.2 %copy-start.3 = (f32[4096]{0:T(1024)S(1)}, f32[4096]{0:T(1024)}, u32[]{:S(2)}) copy-start(f32[4096]{0:T(1024)} %param.21) | copy-start | bytes 49156
  133.3 32.4 %all-to-all-start.2 = ((bf16[16,64,1024]{2,1,0:T(8,128)(2,1)}), bf16[16,64,1024]{2,1,0:T(8,128)(2,1)S(1)}, u32[]{:S(2)}, u32[]{:S(2)}) async-start(bf16[16,64,1024]{2,1,0:T(8,128)(2,1)} %get-tuple-element.130), calls=%async_computation.2 | async-start | bytes 4194304 | tf_op jit(solution)/shard_map/all_to_all | solution.py:40
  174.6 25.0 %all-to-all-start.3 = ((bf16[4,48,4096]{2,1,0:T(8,128)(2,1)}), bf16[4,48,4096]{2,1,0:T(8,128)(2,1)S(1)}, u32[]{:S(2)}, u32[]{:S(2)}) async-start(bf16[4,48,4096]{2,1,0:T(8,128)(2,1)} %bitcast.14), calls=%async_computation.3 | async-start | bytes 3145728 | tf_op jit(solution)/shard_map/all_to_all | solution.py:202
  219.1 23.6 %all-to-all-start.4 = ((bf16[4,1,4,48,1024]{4,3,2,1,0:T(8,128)(2,1)}), bf16[4,1,4,48,1024]{4,3,2,1,0:T(8,128)(2,1)S(1)}, u32[]{:S(2)}, u32[]{:S(2)}) async-start(bf16[4,1,4,48,1024]{4,3,2,1,0:T(8,128)(2,1)} %copy.60), calls=%async_computation.4 | async-start | bytes 3145728 | tf_op jit(solution)/shard_map/all_to_all | solution.py:40
  243.8 11.5 %all-to-all-start.5 = ((bf16[1,4,48,1024]{3,2,0,1:T(8,128)(2,1)}), bf16[1,4,48,1024]{3,2,0,1:T(8,128)(2,1)S(1)}, u32[]{:S(2)}, u32[]{:S(2)}) async-start(bf16[1,4,48,1024]{3,2,0,1:T(8,128)(2,1)} %bitcast.30), calls=%async_computation.5 | async-start | bytes 786432 | tf_op jit(solution)/shard_map/all_to_all | solution.py:204
where the time goes:
time: 260 us; the launch traced here: 258 us
  waiting for transfers between devices  85.2 us (33%)
  matrix products  45.8 us (18%)
  local copies, waits for them, and re-layouts  41.3 us (16%)
  loops' own time  40.3 us (15%)
  starting transfers between devices  26.8 us (10%)
  other arithmetic  11.9 us (5%)
  blocking collectives  6.5 us (2%)
    all_to_all x3, waiting for transfers between devices, sum_at_owner(): lax.all_to_all(blocks, axis, split_axis=0, concat_axis=0, tiled=True)  58.9 us
    another operation x1, loops' own time, shards(): lax.map(pair_term, pair_ids)  40.1 us
    another operation x1, local copies, waits for them, and re-layouts  17.8 us
    dot_general x1, matrix products, expert_ffn(): jnp.einsum('secf,efgq->gsecq', hidden_act, out_blocks, preferred_element_...  16.7 us
    dot_general x16, matrix products, pair_term(): return jnp.dot(row_block, col_block, preferred_element_type=jnp.float32)  15.1 us
    all_to_all x1, waiting for transfers between devices, sent_to_all(): lax.all_to_all(jnp.broadcast_to(value[None], (peers, *value.shape)), axis...  15 us
    all_to_all x3, starting transfers between devices, sum_at_owner(): lax.all_to_all(blocks, axis, split_axis=0, concat_axis=0, tiled=True)  11.7 us
    dynamic_slice x16, local copies, waits for them, and re-layouts, shards(): lax.map(pair_term, pair_ids)  9.44 us
  transfers between devices with their start and end apart: 6, of which 6 were waited for; matrix products, arithmetic and copies ran while one was open for 10% of the time, Pallas kernels for 0%

commit v1 on v0

v1 whole, which is shorter than its diff:
```python
import math

import jax
import jax.numpy as jnp
from jax import lax
from jax.experimental import pallas as pl
from jax.experimental.pallas import tpu as pltpu
from jax.sharding import PartitionSpec as P

HEAD_DIM = 64
MESH = pl.DeviceIdType.MESH


neg_big = -1e30
norm_eps = 1e-06


def in_order(blocks, dim):
    shape = list(blocks.shape[1:])
    shape[dim] *= blocks.shape[0]
    return jnp.moveaxis(blocks, 0, dim).reshape(shape)


def sent_to_all(value, axis):
    peers = lax.axis_size(axis)
    return lax.all_to_all(
        jnp.broadcast_to(value[None], (peers, *value.shape)), axis, 0, 0, tiled=True
    )


def collect(value, axis, dim):
    return in_order(sent_to_all(value, axis), dim)


def in_blocks(value, dim, peers):
    before, after = (value.shape[:dim], value.shape[dim + 1 :])
    return jnp.moveaxis(value.reshape(*before, peers, -1, *after), dim, 0)


def sum_at_owner(value, axis, dim):
    blocks = in_blocks(value, dim, lax.axis_size(axis))
    arrived = lax.all_to_all(blocks, axis, split_axis=0, concat_axis=0, tiled=True)
    return arrived.astype(jnp.float32).sum(axis=0)


def empty_state(row_count, head_count):
    return (
        jnp.full((row_count, head_count), neg_big, jnp.float32),
        jnp.zeros((row_count, head_count), jnp.float32),
        jnp.zeros((row_count, head_count, HEAD_DIM), jnp.float32),
    )


def slot_update(running, query_rows, key_rows, value_rows, is_live):
    run_max, run_sum, run_acc = running
    scores = jnp.einsum(
        "rhd,khd->rhk", query_rows, key_rows, preferred_element_type=jnp.float32
    ) * HEAD_DIM ** (-0.5)
    new_max = jnp.where(is_live[:, None], jnp.maximum(run_max, jnp.max(scores, axis=2)), run_max)
    weights = jnp.where(is_live[:, None, None], jnp.exp(scores - new_max[:, :, None]), 0.0)
    shrink = jnp.exp(run_max - new_max)
    run_sum = run_sum * shrink + jnp.sum(weights, axis=2)
    taken_sum = jnp.einsum(
        "rhk,khd->rhd", weights.astype(jnp.bfloat16), value_rows, preferred_element_type=jnp.float32
    )
    return (new_max, run_sum, run_acc * shrink[:, :, None] + taken_sum)


def slot_scan(running, kv_block, first_slot, query_rows, slot_tags):
    head_count = query_rows.shape[1]

    def visit_slot(carried, element):
        kv_pair, position = element
        key_rows = kv_pair[0].reshape(kv_pair.shape[1], head_count, HEAD_DIM)
        value_rows = kv_pair[1].reshape(kv_pair.shape[1], head_count, HEAD_DIM)
        return (slot_update(carried, query_rows, key_rows, value_rows, slot_tags == position), None)

    positions = first_slot + jnp.arange(kv_block.shape[0], dtype=jnp.int32)
    running, _ = lax.scan(visit_slot, running, (kv_block, positions))
    return running


def finish(running):
    run_max, run_sum, run_acc = running
    safe_sum = jnp.where(run_sum > 0.0, run_sum, 1.0)
    return (run_acc / safe_sum[:, :, None]).reshape(run_acc.shape[0], -1)


def remote(src, dst, sems, slot, target):
    send_sems, recv_sems = sems
    return pltpu.make_async_remote_copy(
        src_ref=src,
        dst_ref=dst,
        send_sem=send_sems.at[slot],
        recv_sem=recv_sems.at[slot],
        device_id=target,
        device_id_type=MESH,
    )


def places():
    y, d = lax.axis_index("narrow"), lax.axis_index("depth")
    x_lo, core = d // 2, d % 2
    return {
        "y": y,
        "d": d,
        "x": x_lo,
        "core": core,
        "up": (y + 1) % 4,
        "down": (y + 3) % 4,
        "far": (y + 2) % 4,
        "mate_d": x_lo * 2 + (1 - core),
        "side_d": (1 - x_lo) * 2 + core,
        "mate_side_d": (1 - x_lo) * 2 + (1 - core),
        "to_mate": {"depth": x_lo * 2 + (1 - core)},
        "to_side": {"depth": (1 - x_lo) * 2 + core},
        "to_up": {"narrow": (y + 1) % 4},
        "to_down": {"narrow": (y + 3) % 4},
    }


def scatter_sum(at, sems, base, part, own, mate_out, mate_in, ring_out, ring_in, side_out, side_in, tile):
    rows_all, quarter = own.shape[1:]
    rows = rows_all // 4
    tiles = quarter // tile

    def rows_of(y):
        return pl.ds(pl.multiple_of(y * rows, rows), rows)

    def fill(target, which, column_block, cast):
        def one(t, _):
            col = pl.multiple_of(column_block * quarter + t * tile, tile)
            here = pl.ds(pl.multiple_of(t * tile, tile), tile)
            target[which, :, here] = cast(part(col))
            return 0

        lax.fori_loop(0, tiles, one, 0)

    bf16 = lambda v: v.astype(jnp.bfloat16)
    mates = [None, None]
    for which, column_block in ((1, at["mate_side_d"]), (0, at["mate_d"])):
        fill(mate_out, which, column_block, bf16)
        mates[which] = remote(mate_out.at[which], mate_in.at[which], sems, base + which, at["to_mate"])
        mates[which].start()
    for which, column_block in ((1, at["side_d"]), (0, at["d"])):
        fill(own, which, column_block, lambda v: v)

    def pair(which, y):
        return own[which, rows_of(y), :] + mate_in[which, rows_of(y), :].astype(jnp.float32)

    def send(slot, value, target):
        ring_out[slot] = bf16(value)
        copy = remote(ring_out.at[slot], ring_in.at[slot], sems, base + 2 + slot, target)
        copy.start()
        return copy

    mates[1].wait_recv()
    copies = [None] * 6
    copies[3] = send(3, pair(1, at["far"]), at["to_down"])
    mates[0].wait_recv()
    copies[0] = send(0, pair(0, at["far"]), at["to_up"])
    copies[1] = send(1, pair(1, at["up"]), at["to_up"])
    copies[4] = send(4, pair(0, at["down"]), at["to_down"])
    copies[3].wait_recv()
    copies[5] = send(5, pair(1, at["down"]) + ring_in[3].astype(jnp.float32), at["to_down"])
    copies[0].wait_recv()
    copies[2] = send(2, pair(0, at["up"]) + ring_in[0].astype(jnp.float32), at["to_up"])
    copies[1].wait_recv()
    copies[5].wait_recv()
    side_out[...] = bf16(pair(1, at["y"]) + ring_in[1].astype(jnp.float32) + ring_in[5].astype(jnp.float32))
    side = remote(side_out, side_in, sems, base + 8, at["to_side"])
    side.start()
    copies[4].wait_recv()
    copies[2].wait_recv()
    mine = pair(0, at["y"]) + ring_in[4].astype(jnp.float32) + ring_in[2].astype(jnp.float32)
    side.wait_recv()
    for copy in [*mates, *copies, side]:
        copy.wait_send()
    return mine + side_in[...].astype(jnp.float32)


def gather_all(at, sems, base, full):
    rows, quarter = full.shape[0] // 4, full.shape[1] // 4
    half = rows // 2

    def block(y, d, part=None):
        cols = pl.ds(pl.multiple_of(d * quarter, quarter), quarter)
        if part is None:
            return full.at[pl.ds(pl.multiple_of(y * rows, rows), rows), cols]
        return full.at[pl.ds(pl.multiple_of(y * rows + part * half, half), half), cols]

    sent = []

    def send(slot, y, d, target, part=None):
        ref = block(y, d, part)
        copy = remote(ref, ref, sems, base + slot, target)
        copy.start()
        sent.append(copy)

    def arrived(slot, y, d, part=None):
        ref = block(y, d, part)
        remote(ref, ref, sems, base + slot, at["to_mate"]).wait_recv()

    y, d, mate, side, mate_side = at["y"], at["d"], at["mate_d"], at["side_d"], at["mate_side_d"]
    up, down, far = at["up"], at["down"], at["far"]
    send(0, y, d, at["to_side"])
    send(1, y, d, at["to_up"])
    send(2, y, d, at["to_down"])
    send(3, y, d, at["to_mate"])
    arrived(0, y, side)
    send(4, y, side, at["to_up"])
    send(5, y, side, at["to_down"])
    send(6, y, side, at["to_mate"])
    arrived(1, down, d)
    send(7, down, d, at["to_up"], 0)
    send(8, down, d, at["to_mate"])
    arrived(2, up, d)
    send(9, up, d, at["to_down"], 1)
    send(10, up, d, at["to_mate"])
    arrived(4, down, side)
    send(11, down, side, at["to_up"], 0)
    send(12, down, side, at["to_mate"])
    arrived(5, up, side)
    send(13, up, side, at["to_down"], 1)
    send(14, up, side, at["to_mate"])
    arrived(7, far, d, 0)
    send(15, far, d, at["to_mate"], 0)
    arrived(9, far, d, 1)
    send(16, far, d, at["to_mate"], 1)
    arrived(11, far, side, 0)
    send(17, far, side, at["to_mate"], 0)
    arrived(13, far, side, 1)
    send(18, far, side, at["to_mate"], 1)
    arrived(3, y, mate)
    arrived(6, y, mate_side)
    arrived(8, down, mate)
    arrived(10, up, mate)
    arrived(12, down, mate_side)
    arrived(14, up, mate_side)
    arrived(15, far, mate, 0)
    arrived(16, far, mate, 1)
    arrived(17, far, mate_side, 0)
    arrived(18, far, mate_side, 1)
    for copy in sent:
        copy.wait_send()


def layer_kernel(
    context,
    hidden_in,
    norm_gain,
    router_parts,
    expert_ids,
    attn_proj_hbm,
    proj_in_hbm,
    proj_out_hbm,
    out,
    attn_proj,
    proj_in,
    proj_out,
    full,
    normed,
    act,
    gate,
    own,
    mate_out,
    mate_in,
    ring_out,
    ring_in,
    side_out,
    side_in,
    load_sems,
    send_sems,
    recv_sems,
):
    at = places()
    sems = (send_sems, recv_sems)
    loads = [
        pltpu.make_async_copy(attn_proj_hbm, attn_proj, load_sems.at[0]),
        pltpu.make_async_copy(proj_in_hbm.at[0], proj_in, load_sems.at[1]),
        pltpu.make_async_copy(proj_out_hbm.at[0], proj_out, load_sems.at[2]),
    ]
    for load in loads:
        load.start()
    barrier = pltpu.get_barrier_semaphore()
    for peer in ("to_mate", "to_side", "to_up", "to_down"):
        pl.semaphore_signal(barrier, inc=1, device_id=at[peer], device_id_type=MESH)
    pl.semaphore_wait(barrier, 4)

    rows, quarter = hidden_in.shape
    tile = min(512, quarter)

    def proj_part(col):
        return jnp.dot(
            context[...], attn_proj[:, pl.ds(col, tile)], preferred_element_type=jnp.float32
        )

    loads[0].wait()
    attn_out = scatter_sum(
        at, sems, 0, proj_part, own, mate_out.at[0], mate_in.at[0], ring_out.at[0], ring_in.at[0],
        side_out.at[0], side_in.at[0], tile,
    )
    my_rows = pl.ds(pl.multiple_of(at["y"] * rows, rows), rows)
    my_cols = pl.ds(pl.multiple_of(at["d"] * quarter, quarter), quarter)
    full[my_rows, my_cols] = (hidden_in[...].astype(jnp.float32) + attn_out).astype(jnp.bfloat16)
    gather_all(at, sems, 9, full)

    strip = 16

    def normalise(s, _):
        here = pl.ds(pl.multiple_of(s * strip, strip), strip)
        value = full[here, :].astype(jnp.float32)
        inv = lax.rsqrt(jnp.mean(value * value, axis=1, keepdims=True) + norm_eps)
        normed[here, :] = (value * inv * norm_gain[...]).astype(jnp.bfloat16)
        return 0

    lax.fori_loop(0, full.shape[0] // strip, normalise, 0)
    logit_parts = lax.dot_general(
        normed[...], router_parts[...], (((1,), (1,)), ((), ())), preferred_element_type=jnp.float32
    )
    ids = expert_ids[...]
    first, second = ids[:, 0:1], ids[:, 1:2]
    chosen = (first == at["y"]) | (second == at["y"])
    other = first + second - at["y"]
    lane = lax.broadcasted_iota(jnp.int32, logit_parts.shape, 1)
    expert_of = lane % 4
    signed = jnp.where(expert_of == at["y"], logit_parts, 0.0) - jnp.where(
        expert_of == other, logit_parts, 0.0
    )
    margin = jnp.sum(signed, axis=1, keepdims=True)
    gate[...] = jnp.where(chosen, 1.0 / (1.0 + jnp.exp(-margin)), 0.0)

    loads[1].wait()
    hidden = act.shape[1]
    step = 256 if hidden % 256 == 0 else hidden

    def first_layer(t, _):
        here = pl.ds(pl.multiple_of(t * step, step), step)
        value = jnp.dot(normed[...], proj_in[:, here], preferred_element_type=jnp.float32)
        act[:, here] = jax.nn.gelu(value, approximate=True).astype(jnp.bfloat16)
        return 0

    lax.fori_loop(0, hidden // step, first_layer, 0)
    loads[2].wait()

    def expert_part(col):
        return gate[...] * jnp.dot(
            act[...], proj_out[:, pl.ds(col, tile)], preferred_element_type=jnp.float32
        )

    combined = scatter_sum(
        at, sems, 28, expert_part, own, mate_out.at[1], mate_in.at[1], ring_out.at[1], ring_in.at[1],
        side_out.at[1], side_in.at[1], tile,
    )
    out[...] = (full[my_rows, my_cols].astype(jnp.float32) + combined).astype(jnp.bfloat16)


def layer_tail(context, hidden_in, norm_gain, router_proj, expert_ids, attn_proj, proj_in, proj_out):
    rows_all, inner = context.shape
    rows, quarter = hidden_in.shape
    width = attn_proj.shape[1]
    hidden = proj_in.shape[2]
    router_rows = router_proj.T
    high = lax.reduce_precision(router_rows, 8, 7)
    middle = lax.reduce_precision(router_rows - high, 8, 7)
    low = router_rows - high - middle
    router_parts = jnp.concatenate([high, middle, low, jnp.zeros_like(low)], axis=0).astype(jnp.bfloat16)
    vmem, hbm = pl.BlockSpec(memory_space=pltpu.VMEM), pl.BlockSpec(memory_space=pl.ANY)
    bf16 = jnp.bfloat16
    copies = 37
    return pl.pallas_call(
        layer_kernel,
        out_shape=jax.ShapeDtypeStruct((rows, quarter), bf16),
        in_specs=[vmem] * 5 + [hbm] * 3,
        out_specs=vmem,
        scratch_shapes=[
            pltpu.VMEM((inner, width), bf16),
            pltpu.VMEM((width, hidden), bf16),
            pltpu.VMEM((hidden, width), bf16),
            pltpu.VMEM((rows_all, width), bf16),
            pltpu.VMEM((rows_all, width), bf16),
            pltpu.VMEM((rows_all, hidden), bf16),
            pltpu.VMEM((rows_all, 1), jnp.float32),
            pltpu.VMEM((2, rows_all, quarter), jnp.float32),
            pltpu.VMEM((2, 2, rows_all, quarter), bf16),
            pltpu.VMEM((2, 2, rows_all, quarter), bf16),
            pltpu.VMEM((2, 6, rows, quarter), bf16),
            pltpu.VMEM((2, 6, rows, quarter), bf16),
            pltpu.VMEM((2, rows, quarter), bf16),
            pltpu.VMEM((2, rows, quarter), bf16),
            pltpu.SemaphoreType.DMA((3,)),
            pltpu.SemaphoreType.DMA((copies,)),
            pltpu.SemaphoreType.DMA((copies,)),
        ],
        compiler_params=pltpu.CompilerParams(
            collective_id=0, has_side_effects=True, vmem_limit_bytes=60 * 1024 * 1024
        ),
        name="layer_tail",
    )(context, hidden_in, norm_gain.reshape(1, -1), router_parts, expert_ids, attn_proj, proj_in, proj_out)


def shards(
    hidden_in,
    queries,
    lang_ids,
    owner_slot,
    enc_kv,
    attn_proj,
    norm_gain,
    router_proj,
    expert_ids,
    proj_in,
    proj_out,
):
    head_count = queries.shape[1] // HEAD_DIM
    lang_count = owner_slot.shape[0]
    lang_match = lang_ids[:, None] == jnp.arange(lang_count, dtype=jnp.int32)[None, :]
    holder = jnp.sum(jnp.where(lang_match, owner_slot[None, :], 0), axis=1)
    first_slot = lax.axis_index("wide") * enc_kv.shape[0]
    segment = collect(queries, "wide", 0)
    row_count = segment.shape[0]
    block_rows = math.gcd(row_count, 512)

    def one_block(element):
        part_rows, part_tags = element
        running = slot_scan(
            empty_state(block_rows, head_count),
            enc_kv,
            first_slot,
            part_rows.reshape(block_rows, head_count, HEAD_DIM),
            part_tags,
        )
        return finish(running)

    blocks_out = lax.map(
        one_block,
        (
            segment.reshape(row_count // block_rows, block_rows, segment.shape[1]),
            holder.reshape(row_count // block_rows, block_rows),
        ),
    )
    partial_context = blocks_out.reshape(row_count, segment.shape[1])
    context = sum_at_owner(partial_context.astype(jnp.bfloat16), "wide", 0).astype(jnp.bfloat16)
    return layer_tail(
        context, hidden_in, norm_gain, router_proj, expert_ids, attn_proj, proj_in, proj_out
    )


def solution(mesh):
    return jax.shard_map(
        shards,
        mesh=mesh,
        in_specs=(
            P(("wide", "narrow"), "depth"),
            P("wide", ("narrow", "depth")),
            P(),
            P(),
            P("wide", None, None, ("narrow", "depth")),
            P(("narrow", "depth"), None),
            P(),
            P(),
            P("wide", None),
            P("narrow", None, "depth"),
            P("narrow", "depth", None),
        ),
        out_specs=P(("wide", "narrow"), "depth"),
        check_vma=False,
    )
```

time: 260 us -> 136 us (0.52)
  Pallas kernels: 0 us -> 63.2 us
  waiting for transfers between devices: 85.2 us -> 29.8 us
  loops' own time: 40.3 us -> 0.2 us
  matrix products: 45.8 us -> 11.6 us
  local copies, waits for them, and re-layouts: 41.3 us -> 10.2 us
  starting transfers between devices: 26.8 us -> 11.4 us
  blocking collectives: 6.5 us -> 0 us
  other arithmetic: 11.9 us -> 9.29 us
    pallas_call x0 -> x1, Pallas kernels: none -> 63.2 us  [layer_tail(): pl.pallas_call(layer_kernel, out_shape=jax.ShapeDtypeStruct((rows, quarte...]
    all_to_all x3 -> x1, waiting for transfers between devices: 58.9 us -> 14.9 us  [sum_at_owner(): lax.all_to_all(blocks, axis, split_axis=0, concat_axis=0, tiled=True)]
    another operation x1 -> x0, loops' own time: 40.1 us -> none  [shards(): lax.map(pair_term, pair_ids)]
    dot_general x19 -> x0, matrix products: 34.2 us -> none  [the longest x1 16.7 us: expert_ffn(): jnp.einsum('secf,efgq->gsecq', hidden_act, out_blocks, preferred_element_...]
    another operation x1 -> x0, local copies, waits for them, and re-layouts: 17.8 us -> none
    all_to_all x2 -> x0, waiting for transfers between devices: 11.3 us -> none  [the longest x1 7.86 us: shards(): lax.all_to_all(summed.astype(jnp.bfloat16), 'narrow', split_axis=1, conca...]
    dynamic_slice x18 -> x0, local copies, waits for them, and re-layouts: 9.62 us -> none  [the longest x16 9.44 us: shards(): lax.map(pair_term, pair_ids)]
    all_to_all x3 -> x1, starting transfers between devices: 11.7 us -> 3.56 us  [sum_at_owner(): lax.all_to_all(blocks, axis, split_axis=0, concat_axis=0, tiled=True)]
  transfers between devices with their start and end apart: 6 -> 2, of which waited for: 6 -> 2; matrix products, arithmetic and copies ran while one was open for 10% -> 3% of each run, Pallas kernels for 0% -> 0%
where the time goes in v1:
time: 136 us
  Pallas kernels  63.2 us (46%)
  waiting for transfers between devices  29.8 us (22%)
  matrix products  11.6 us (9%)
  starting transfers between devices  11.4 us (8%)
  local copies, waits for them, and re-layouts  10.2 us (7%)
  other arithmetic  9.29 us (7%)
    pallas_call x1, Pallas kernels, layer_tail(): pl.pallas_call(layer_kernel, out_shape=jax.ShapeDtypeStruct((rows, quarte...  63.2 us
    all_to_all x1, waiting for transfers between devices, sent_to_all(): lax.all_to_all(jnp.broadcast_to(value[None], (peers, *value.shape)), axis...  15 us
    all_to_all x1, waiting for transfers between devices, sum_at_owner(): lax.all_to_all(blocks, axis, split_axis=0, concat_axis=0, tiled=True)  14.9 us
    all_to_all x1, starting transfers between devices, sent_to_all(): lax.all_to_all(jnp.broadcast_to(value[None], (peers, *value.shape)), axis...  7.89 us
    dot_general x4, matrix products, slot_update(): jnp.einsum('rhk,khd->rhd', weights.astype(jnp.bfloat16), value_rows, pref...  7.1 us
    reduce_sum x4, other arithmetic, slot_update(): run_sum = run_sum * shrink + jnp.sum(weights, axis=2)  6.68 us
    dot_general x4, matrix products, slot_update(): jnp.einsum('rhd,khd->rhk', query_rows, key_rows, preferred_element_type=j...  4.47 us
    all_to_all x1, starting transfers between devices, sum_at_owner(): lax.all_to_all(blocks, axis, split_axis=0, concat_axis=0, tiled=True)  3.56 us
  transfers between devices with their start and end apart: 2, of which 2 were waited for; matrix products, arithmetic and copies ran while one was open for 3% of the time, Pallas kernels for 0%

profile of v1, /device:TPU:0, one launch (start us, length us, event | category | flops | bytes accessed | tf_op | source)
XLA Modules:
  0.0 135.8 jit_solution(16420856542454772700)
XLA Ops:
  0.0 2.0 %broadcast_in_dim.74 = bf16[8,256,256]{2,1,0:T(8,128)(2,1)} broadcast(bf16[256,256]{1,0:T(8,128)(2,1)} %param.14), dimensions={1,2} | broadcast | bytes 1179648 | tf_op jit(solution)/shard_map/broadcast_in_dim | solution.py:27
  2.0 7.9 %all-to-all-start = ((bf16[8,256,256]{2,1,0:T(8,128)(2,1)}), bf16[8,256,256]{2,1,0:T(8,128)(2,1)S(1)}, u32[]{:S(2)}, u32[]{:S(2)}) async-start(bf16[8,256,256]{2,1,0:T(8,128)(2,1)} %broadcast_in_dim.74), calls=%async_computation | async-start | bytes 2097152 | tf_op jit(solution)/shard_map/all_to_all | solution.py:26
  9.9 0.8 select_reduce_fusion
  10.7 1.4 %copy.19 = bf16[1,2,768,256]{2,3,1,0:T(8,128)(2,1)S(1)} copy(bf16[1,2,768,256]{3,2,1,0:T(8,128)(2,1)} %param.17) | data formatting | bytes 1572864 | tf_op jit(solution)/shard_map/while | solution.py:435
  12.1 15.0 %all-to-all-done = bf16[8,256,256]{2,1,0:T(8,128)(2,1)S(1)} async-done(((bf16[8,256,256]{2,1,0:T(8,128)(2,1)}), bf16[8,256,256]{2,1,0:T(8,128)(2,1)S(1)}, u32[]{:S(2)}, u32[]{:S(2)}) %all-to-all-start) | async-done | bytes 1048608 | tf_op jit(solution)/shard_map/all_to_all | solution.py:26
  27.1 23.0 %while.12 = (s32[]{:T(128)}, bf16[4,512,256]{2,1,0:T(8,128)(2,1)}, s32[4,512]{1,0:T(4,128)S(1)}, s32[]{:T(128)}, bf16[4,512,256]{2,1,0:T(8,128)(2,1)S(1)}, /*index=5*/bf16[1,2,768,256]{2,3,1,0:T(8,128)(2,1)S(1)}, s32[]{:T(128)}) while((s32[]{:T(128)}, bf16[4,512,256]{2,1,0:T(8,128)(2,1)}, s32[4,512]{1,0:T(4,128)S(1)}, s32[]{:T(128)}, ...), condition=%wide.region_4.5_spmd, body=%wide.region_1.4_spmd.sunk | while | flops 418789888 | bytes 23957604 | solution.py:435
  27.3 1.1 bitcast_reduce_fusion.2
  28.5 1.7 %fusion.35 = f32[512,4]{0,1:T(4,128)S(1)} fusion(f32[4,512,768]{2,1,0:T(8,128)S(1)} %get-tuple-element.146, f32[512,4]{0,1:T(4,128)S(1)} %get-tuple-element.148, pred[512]{0:T(512)(128)(4,1)S(1)} %compare_reduce_fusion.2), kind=kLoop, calls=%fused_computation.4.clone.1 | loop fusion | flops 6289408 | bytes 6308352 | tf_op jit(solution)/shard_map/while/body/eval_jaxpr/while/body/eval_jaxpr/reduce_sum | solution.py:62
  30.2 1.8 %fusion.36 = bf16[512,4,64]{0,2,1:T(8,128)(2,1)S(1)} fusion(bf16[768,4,64]{0,2,1:T(8,128)(2,1)S(1)} %bitcast.65, f32[4,512,768]{2,1,0:T(8,128)S(1)} %get-tuple-element.146, f32[512,4]{0,1:T(4,128)S(1)} %get-tuple-element.148, pred[512]{0:T(512)(128)(4,1)S(1)} %compare_reduce_fusion.2, f32[512,4]{0,1:T(4,128)S(1)} %compare_select_fusion.2, ...), kind=kOutput, calls=%fused_computation.10.clone.1 | convolution fusion | flops 208011264 | bytes 6971904 | tf_op jit(solution)/shard_map/while/body/eval_jaxpr/while/body/eval_jaxpr/rhk,khd->rhd/dot_general | solution.py:63
  33.1 1.1 bitcast_reduce_fusion.2
  34.2 1.7 %fusion.35 = f32[512,4]{0,1:T(4,128)S(1)} fusion(f32[4,512,768]{2,1,0:T(8,128)S(1)} %get-tuple-element.146, f32[512,4]{0,1:T(4,128)S(1)} %get-tuple-element.148, pred[512]{0:T(512)(128)(4,1)S(1)} %compare_reduce_fusion.2), kind=kLoop, calls=%fused_computation.4.clone.1 | loop fusion | flops 6289408 | bytes 6308352 | tf_op jit(solution)/shard_map/while/body/eval_jaxpr/while/body/eval_jaxpr/reduce_sum | solution.py:62
  35.9 1.8 %fusion.36 = bf16[512,4,64]{0,2,1:T(8,128)(2,1)S(1)} fusion(bf16[768,4,64]{0,2,1:T(8,128)(2,1)S(1)} %bitcast.65, f32[4,512,768]{2,1,0:T(8,128)S(1)} %get-tuple-element.146, f32[512,4]{0,1:T(4,128)S(1)} %get-tuple-element.148, pred[512]{0:T(512)(128)(4,1)S(1)} %compare_reduce_fusion.2, f32[512,4]{0,1:T(4,128)S(1)} %compare_select_fusion.2, ...), kind=kOutput, calls=%fused_computation.10.clone.1 | convolution fusion | flops 208011264 | bytes 6971904 | tf_op jit(solution)/shard_map/while/body/eval_jaxpr/while/body/eval_jaxpr/rhk,khd->rhd/dot_general | solution.py:63
  38.8 1.1 bitcast_reduce_fusion.2
  40.0 1.7 %fusion.35 = f32[512,4]{0,1:T(4,128)S(1)} fusion(f32[4,512,768]{2,1,0:T(8,128)S(1)} %get-tuple-element.146, f32[512,4]{0,1:T(4,128)S(1)} %get-tuple-element.148, pred[512]{0:T(512)(128)(4,1)S(1)} %compare_reduce_fusion.2), kind=kLoop, calls=%fused_computation.4.clone.1 | loop fusion | flops 6289408 | bytes 6308352 | tf_op jit(solution)/shard_map/while/body/eval_jaxpr/while/body/eval_jaxpr/reduce_sum | solution.py:62
  41.7 1.8 %fusion.36 = bf16[512,4,64]{0,2,1:T(8,128)(2,1)S(1)} fusion(bf16[768,4,64]{0,2,1:T(8,128)(2,1)S(1)} %bitcast.65, f32[4,512,768]{2,1,0:T(8,128)S(1)} %get-tuple-element.146, f32[512,4]{0,1:T(4,128)S(1)} %get-tuple-element.148, pred[512]{0:T(512)(128)(4,1)S(1)} %compare_reduce_fusion.2, f32[512,4]{0,1:T(4,128)S(1)} %compare_select_fusion.2, ...), kind=kOutput, calls=%fused_computation.10.clone.1 | convolution fusion | flops 208011264 | bytes 6971904 | tf_op jit(solution)/shard_map/while/body/eval_jaxpr/while/body/eval_jaxpr/rhk,khd->rhd/dot_general | solution.py:63
  44.6 1.1 bitcast_reduce_fusion.2
  45.7 1.7 %fusion.35 = f32[512,4]{0,1:T(4,128)S(1)} fusion(f32[4,512,768]{2,1,0:T(8,128)S(1)} %get-tuple-element.146, f32[512,4]{0,1:T(4,128)S(1)} %get-tuple-element.148, pred[512]{0:T(512)(128)(4,1)S(1)} %compare_reduce_fusion.2), kind=kLoop, calls=%fused_computation.4.clone.1 | loop fusion | flops 6289408 | bytes 6308352 | tf_op jit(solution)/shard_map/while/body/eval_jaxpr/while/body/eval_jaxpr/reduce_sum | solution.py:62
  47.4 1.8 %fusion.36 = bf16[512,4,64]{0,2,1:T(8,128)(2,1)S(1)} fusion(bf16[768,4,64]{0,2,1:T(8,128)(2,1)S(1)} %bitcast.65, f32[4,512,768]{2,1,0:T(8,128)S(1)} %get-tuple-element.146, f32[512,4]{0,1:T(4,128)S(1)} %get-tuple-element.148, pred[512]{0:T(512)(128)(4,1)S(1)} %compare_reduce_fusion.2, f32[512,4]{0,1:T(4,128)S(1)} %compare_select_fusion.2, ...), kind=kOutput, calls=%fused_computation.10.clone.1 | convolution fusion | flops 208011264 | bytes 6971904 | tf_op jit(solution)/shard_map/while/body/eval_jaxpr/while/body/eval_jaxpr/rhk,khd->rhd/dot_general | solution.py:63
  50.1 3.6 %all-to-all-start.1 = ((bf16[8,256,256]{2,1,0:T(8,128)(2,1)}), bf16[8,256,256]{2,1,0:T(8,128)(2,1)S(1)}, u32[]{:S(2)}, u32[]{:S(2)}) async-start(bf16[8,256,256]{2,1,0:T(8,128)(2,1)} %bitcast.68), calls=%async_computation.1 | async-start | bytes 2097152 | tf_op jit(solution)/shard_map/all_to_all | solution.py:42
  53.7 0.8 copy.21.expert_ids
  55.3 14.9 %all-to-all-done.1 = bf16[8,256,256]{2,1,0:T(8,128)(2,1)S(1)} async-done(((bf16[8,256,256]{2,1,0:T(8,128)(2,1)}), bf16[8,256,256]{2,1,0:T(8,128)(2,1)S(1)}, u32[]{:S(2)}, u32[]{:S(2)}) %all-to-all-start.1) | async-done | bytes 1048608 | tf_op jit(solution)/shard_map/all_to_all | solution.py:42
  70.2 0.8 reduce_sum.32.context
  71.0 63.2 %layer_tail.1 = bf16[64,1024]{1,0:T(8,128)(2,1)} custom-call(bf16[256,256]{1,0:T(8,128)(2,1)} %reduce_sum.32.context, bf16[64,1024]{1,0:T(8,128)(2,1)} %hidden_in.1, f32[1,4096]{1,0:T(1,128)} %bitcast.69, bf16[16,4096]{1,0:T(8,128)(2,1)} %maximum_maximum_fusion.router_parts, s32[256,2]{1,0:T(8,128)} %copy.21.expert_ids, bf16[256,4096]{1,0:T(8,128)(2,1)} %attn_proj_hbm.1, ...), custom_call_target="tpu_custom_call" | custom-call | tf_op jit(solution)/shard_map/layer_tail/pallas_call | solution.py:371
  134.2 1.6 %copy.39 = bf16[64,1024]{1,0:T(8,128)(2,1)} copy(bf16[64,1024]{1,0:T(8,128)(2,1)} %layer_tail.1) | data formatting | bytes 262144
  (42 shorter events, 5.4 us)
Async XLA Ops:
  2.0 25.1 %all-to-all-start = ((bf16[8,256,256]{2,1,0:T(8,128)(2,1)}), bf16[8,256,256]{2,1,0:T(8,128)(2,1)S(1)}, u32[]{:S(2)}, u32[]{:S(2)}) async-start(bf16[8,256,256]{2,1,0:T(8,128)(2,1)} %broadcast_in_dim.74), calls=%async_computation | async-start | bytes 2097152 | tf_op jit(solution)/shard_map/all_to_all | solution.py:26
  27.1 26.6 %copy-start = (f32[4096,4]{0,1:T(4,128)S(1)}, f32[4096,4]{0,1:T(4,128)}, u32[]{:S(2)}) copy-start(f32[4096,4]{0,1:T(4,128)} %param.20) | copy-start | bytes 196612
  27.1 26.6 %copy-start.1 = (s32[256,2]{0,1:T(2,128)S(1)}, s32[256,2]{0,1:T(2,128)}, u32[]{:S(2)}) copy-start(s32[256,2]{0,1:T(2,128)} %param.21) | copy-start | bytes 6148
  50.1 20.1 %all-to-all-start.1 = ((bf16[8,256,256]{2,1,0:T(8,128)(2,1)}), bf16[8,256,256]{2,1,0:T(8,128)(2,1)S(1)}, u32[]{:S(2)}, u32[]{:S(2)}) async-start(bf16[8,256,256]{2,1,0:T(8,128)(2,1)} %bitcast.68), calls=%async_computation.1 | async-start | bytes 2097152 | tf_op jit(solution)/shard_map/all_to_all | solution.py:42

commit v2 on v1

--- a/solution.py
+++ b/solution.py
@@ -11,79 +11,7 @@
 MESH = pl.DeviceIdType.MESH
 
 
-neg_big = -1e30
 norm_eps = 1e-06
-
-
-def in_order(blocks, dim):
-    shape = list(blocks.shape[1:])
-    shape[dim] *= blocks.shape[0]
-    return jnp.moveaxis(blocks, 0, dim).reshape(shape)
-
-
-def sent_to_all(value, axis):
-    peers = lax.axis_size(axis)
-    return lax.all_to_all(
-        jnp.broadcast_to(value[None], (peers, *value.shape)), axis, 0, 0, tiled=True
-    )
-
-
-def collect(value, axis, dim):
-    return in_order(sent_to_all(value, axis), dim)
-
-
-def in_blocks(value, dim, peers):
-    before, after = (value.shape[:dim], value.shape[dim + 1 :])
-    return jnp.moveaxis(value.reshape(*before, peers, -1, *after), dim, 0)
-
-
-def sum_at_owner(value, axis, dim):
-    blocks = in_blocks(value, dim, lax.axis_size(axis))
-    arrived = lax.all_to_all(blocks, axis, split_axis=0, concat_axis=0, tiled=True)
-    return arrived.astype(jnp.float32).sum(axis=0)
-
-
-def empty_state(row_count, head_count):
-    return (
-        jnp.full((row_count, head_count), neg_big, jnp.float32),
-        jnp.zeros((row_count, head_count), jnp.float32),
-        jnp.zeros((row_count, head_count, HEAD_DIM), jnp.float32),
-    )
-
-
-def slot_update(running, query_rows, key_rows, value_rows, is_live):
-    run_max, run_sum, run_acc = running
-    scores = jnp.einsum(
-        "rhd,khd->rhk", query_rows, key_rows, preferred_element_type=jnp.float32
-    ) * HEAD_DIM ** (-0.5)
-    new_max = jnp.where(is_live[:, None], jnp.maximum(run_max, jnp.max(scores, axis=2)), run_max)
-    weights = jnp.where(is_live[:, None, None], jnp.exp(scores - new_max[:, :, None]), 0.0)
-    shrink = jnp.exp(run_max - new_max)
-    run_sum = run_sum * shrink + jnp.sum(weights, axis=2)
-    taken_sum = jnp.einsum(
-        "rhk,khd->rhd", weights.astype(jnp.bfloat16), value_rows, preferred_element_type=jnp.float32
-    )
-    return (new_max, run_sum, run_acc * shrink[:, :, None] + taken_sum)
-
-
-def slot_scan(running, kv_block, first_slot, query_rows, slot_tags):
-    head_count = query_rows.shape[1]
-
-    def visit_slot(carried, element):
-        kv_pair, position = element
-        key_rows = kv_pair[0].reshape(kv_pair.shape[1], head_count, HEAD_DIM)
-        value_rows = kv_pair[1].reshape(kv_pair.shape[1], head_count, HEAD_DIM)
-        return (slot_update(carried, query_rows, key_rows, value_rows, slot_tags == position), None)
-
-    positions = first_slot + jnp.arange(kv_block.shape[0], dtype=jnp.int32)
-    running, _ = lax.scan(visit_slot, running, (kv_block, positions))
-    return running
-
-
-def finish(running):
-    run_max, run_sum, run_acc = running
-    safe_sum = jnp.where(run_sum > 0.0, run_sum, 1.0)
-    return (run_acc / safe_sum[:, :, None]).reshape(run_acc.shape[0], -1)
 
 
 def remote(src, dst, sems, slot, target):
@@ -245,16 +173,146 @@
         copy.wait_send()
 
 
+def wide_places():
+    w = lax.axis_index("wide")
+    z, x = w // 2, w % 2
+    up, down, far = (z + 1) % 4, (z + 3) % 4, (z + 2) % 4
+    order = [z * 2 + x, up * 2 + x, down * 2 + x, z * 2 + 1 - x, far * 2 + x, up * 2 + 1 - x, down * 2 + 1 - x, far * 2 + 1 - x]
+    return {"w": w, "order": order}
+
+
+OWN, UP, DOWN, SIDE, FAR, UP_SIDE, DOWN_SIDE, FAR_SIDE = range(8)
+BACK = (OWN, DOWN, UP, SIDE, FAR, DOWN_SIDE, UP_SIDE, FAR_SIDE)
+
+
+def attend(at, sems, base, lang_rows, owner_slot, asked, keys, values, marks, answer, returned, context):
+    rows, feats = context.shape
+    heads = feats // HEAD_DIM
+    length = keys.shape[2]
+    half = rows // 2
+    order = at["order"]
+
+    def send(slot, src_slot, dst_slot, target_slot, part=None):
+        src, dst = asked.at[src_slot], asked.at[dst_slot]
+        if part is not None:
+            here = pl.ds(part * half, half)
+            src, dst = asked.at[src_slot, here], asked.at[dst_slot, here]
+        remote(src, dst, sems, base + slot, {"wide": order[target_slot]}).start()
+
+    def arrived(slot, dst_slot, part=None):
+        dst = asked.at[dst_slot] if part is None else asked.at[dst_slot, pl.ds(part * half, half)]
+        remote(dst, dst, sems, base + slot, {"wide": order[SIDE]}).wait_recv()
+
+    send(0, OWN, SIDE, SIDE)
+    send(1, OWN, DOWN, UP)
+    send(2, OWN, UP, DOWN)
+
+    group = jnp.int32(0)
+    for g in range(owner_slot.shape[0]):
+        group = group + jnp.where(owner_slot[g] == at["w"], g, 0)
+    marks[...] = jnp.where(lang_rows[...] == group, 1.0, 0.0).T
+    scale = HEAD_DIM ** (-0.5) * math.log2(math.e)
+
+    def one_block(k, _):
+        @pl.when(k == UP)
+        def _():
+            arrived(1, DOWN)
+            send(3, DOWN, FAR, UP, 0)
+            arrived(2, UP)
+            send(4, UP, FAR, DOWN, 1)
+
+        @pl.when(k == DOWN)
+        def _():
+            arrived(0, SIDE)
+            send(5, SIDE, DOWN_SIDE, UP)
+            send(6, SIDE, UP_SIDE, DOWN)
+
+        @pl.when(k == FAR)
+        def _():
+            arrived(3, FAR, 0)
+            arrived(4, FAR, 1)
+            arrived(5, DOWN_SIDE)
+            send(7, DOWN_SIDE, FAR_SIDE, UP, 0)
+            arrived(6, UP_SIDE)
+            send(8, UP_SIDE, FAR_SIDE, DOWN, 1)
+
+        @pl.when(k == FAR_SIDE)
+        def _():
+            arrived(7, FAR_SIDE, 0)
+            arrived(8, FAR_SIDE, 1)
+
+        source = jnp.int32(0)
+        for slot in range(8):
+            source = source + jnp.where(k == slot, order[slot], 0)
+        lane = lax.broadcasted_iota(jnp.int32, marks.shape, 1)
+        here = jnp.sum(jnp.where(lane == source, marks[...], 0.0), axis=1, keepdims=True)
+        query = asked[k]
+        total = jnp.zeros((rows, feats), jnp.float32)
+        for head in range(heads):
+            scores = jnp.dot(query, keys[head], preferred_element_type=jnp.float32)
+            top = jnp.max(scores, axis=1, keepdims=True)
+            weights = jnp.exp2((scores - top) * scale)
+            below = jnp.sum(weights, axis=1, keepdims=True)
+            taken = jnp.dot(weights.astype(jnp.bfloat16), values[head], preferred_element_type=jnp.float32)
+            total = total + taken * (here / below)
+        answer[k] = total.astype(jnp.bfloat16)
+        for slot in range(1, 8):
+
+            @pl.when(k == slot)
+            def _():
+                remote(
+                    answer.at[slot], returned.at[BACK[slot]], sems, base + 8 + slot, {"wide": order[slot]}
+                ).start()
+
+        return 0
+
+    lax.fori_loop(0, 8, one_block, 0)
+    summed = answer[OWN].astype(jnp.float32)
+    for slot in range(1, 8):
+        remote(answer.at[slot], returned.at[BACK[slot]], sems, base + 8 + slot, {"wide": order[slot]}).wait_recv()
+    for slot in range(1, 8):
+        summed = summed + returned[slot].astype(jnp.float32)
+    context[...] = summed.astype(jnp.bfloat16)
+    for slot in range(9):
+        part = slot in (3, 4, 7, 8)
+        src = asked.at[OWN, pl.ds(0, half)] if part else asked.at[OWN]
+        remote(src, src, sems, base + slot, {"wide": order[SIDE]}).wait_send()
+    for slot in range(1, 8):
+        remote(answer.at[slot], returned.at[BACK[slot]], sems, base + 8 + slot, {"wide": order[slot]}).wait_send()
+
+
+def spread_heads(kv, keys, values):
+    heads = keys.shape[0]
+    flipped = kv[0].T
+    plain = kv[1]
+    for head in range(heads):
+        place = lax.broadcasted_iota(jnp.int32, flipped.shape, 0) // HEAD_DIM
+        keys[head] = jnp.where(place == head, flipped, jnp.zeros_like(flipped))
+        place = lax.broadcasted_iota(jnp.int32, plain.shape, 1) // HEAD_DIM
+        values[head] = jnp.where(place == head, plain, jnp.zeros_like(plain))
+
+
 def layer_kernel(
-    context,
+    owner_slot,
+    lang_rows,
     hidden_in,
     norm_gain,
     router_parts,
     expert_ids,
+    queries_hbm,
+    enc_kv_hbm,
     attn_proj_hbm,
     proj_in_hbm,
     proj_out_hbm,
     out,
+    asked,
+    kv,
+    keys,
+    values,
+    marks,
+    answer,
+    returned,
+    context,
     attn_proj,
     proj_in,
     proj_out,
@@ -275,6 +333,11 @@
 ):
     at = places()
     sems = (send_sems, recv_sems)
+    wide_at = wide_places()
+    query_load = pltpu.make_async_copy(queries_hbm, asked.at[OWN], load_sems.at[3])
+    query_load.start()
+    kv_load = pltpu.make_async_copy(enc_kv_hbm.at[0], kv, load_sems.at[4])
+    kv_load.start()
     loads = [
         pltpu.make_async_copy(attn_proj_hbm, attn_proj, load_sems.at[0]),
         pltpu.make_async_copy(proj_in_hbm.at[0], proj_in, load_sems.at[1]),
@@ -285,7 +348,16 @@
     barrier = pltpu.get_barrier_semaphore()
     for peer in ("to_mate", "to_side", "to_up", "to_down"):
         pl.semaphore_signal(barrier, inc=1, device_id=at[peer], device_id_type=MESH)
-    pl.semaphore_wait(barrier, 4)
+    for slot in range(1, 8):
+        peer = {"wide": wide_at["order"][slot]}
+        pl.semaphore_signal(barrier, inc=1, device_id=peer, device_id_type=MESH)
+    kv_load.wait()
+    spread_heads(kv, keys, values)
+    query_load.wait()
+    pl.semaphore_wait(barrier, 11)
+    attend(
+        wide_at, sems, 37, lang_rows, owner_slot, asked, keys, values, marks, answer, returned, context
+    )
 
     rows, quarter = hidden_in.shape
     tile = min(512, quarter)
@@ -355,11 +427,25 @@
     out[...] = (full[my_rows, my_cols].astype(jnp.float32) + combined).astype(jnp.bfloat16)
 
 
-def layer_tail(context, hidden_in, norm_gain, router_proj, expert_ids, attn_proj, proj_in, proj_out):
-    rows_all, inner = context.shape
+def layer_step(
+    hidden_in,
+    queries,
+    lang_ids,
+    owner_slot,
+    enc_kv,
+    attn_proj,
+    norm_gain,
+    router_proj,
+    expert_ids,
+    proj_in,
+    proj_out,
+):
+    rows_all, inner = queries.shape
     rows, quarter = hidden_in.shape
     width = attn_proj.shape[1]
     hidden = proj_in.shape[2]
+    length = enc_kv.shape[2]
+    heads = inner // HEAD_DIM
     router_rows = router_proj.T
     high = lax.reduce_precision(router_rows, 8, 7)
     middle = lax.reduce_precision(router_rows - high, 8, 7)
@@ -367,13 +453,21 @@
     router_parts = jnp.concatenate([high, middle, low, jnp.zeros_like(low)], axis=0).astype(jnp.bfloat16)
     vmem, hbm = pl.BlockSpec(memory_space=pltpu.VMEM), pl.BlockSpec(memory_space=pl.ANY)
     bf16 = jnp.bfloat16
-    copies = 37
+    copies = 37 + 16
     return pl.pallas_call(
         layer_kernel,
         out_shape=jax.ShapeDtypeStruct((rows, quarter), bf16),
-        in_specs=[vmem] * 5 + [hbm] * 3,
+        in_specs=[pl.BlockSpec(memory_space=pltpu.SMEM)] + [vmem] * 5 + [hbm] * 5,
         out_specs=vmem,
         scratch_shapes=[
+            pltpu.VMEM((8, rows_all, inner), bf16),
+            pltpu.VMEM((2, length, inner), bf16),
+            pltpu.VMEM((heads, inner, length), bf16),
+            pltpu.VMEM((heads, length, inner), bf16),
+            pltpu.VMEM((rows_all, 8), jnp.float32),
+            pltpu.VMEM((8, rows_all, inner), bf16),
+            pltpu.VMEM((8, rows_all, inner), bf16),
+            pltpu.VMEM((rows_all, inner), bf16),
             pltpu.VMEM((inner, width), bf16),
             pltpu.VMEM((width, hidden), bf16),
             pltpu.VMEM((hidden, width), bf16),
@@ -388,67 +482,32 @@
             pltpu.VMEM((2, 6, rows, quarter), bf16),
             pltpu.VMEM((2, rows, quarter), bf16),
             pltpu.VMEM((2, rows, quarter), bf16),
-            pltpu.SemaphoreType.DMA((3,)),
+            pltpu.SemaphoreType.DMA((5,)),
             pltpu.SemaphoreType.DMA((copies,)),
             pltpu.SemaphoreType.DMA((copies,)),
         ],
         compiler_params=pltpu.CompilerParams(
             collective_id=0, has_side_effects=True, vmem_limit_bytes=60 * 1024 * 1024
         ),
-        name="layer_tail",
-    )(context, hidden_in, norm_gain.reshape(1, -1), router_parts, expert_ids, attn_proj, proj_in, proj_out)
-
-
-def shards(
-    hidden_in,
-    queries,
-    lang_ids,
-    owner_slot,
-    enc_kv,
-    attn_proj,
-    norm_gain,
-    router_proj,
-    expert_ids,
-    proj_in,
-    proj_out,
-):
-    head_count = queries.shape[1] // HEAD_DIM
-    lang_count = owner_slot.shape[0]
-    lang_match = lang_ids[:, None] == jnp.arange(lang_count, dtype=jnp.int32)[None, :]
-    holder = jnp.sum(jnp.where(lang_match, owner_slot[None, :], 0), axis=1)
-    first_slot = lax.axis_index("wide") * enc_kv.shape[0]
-    segment = collect(queries, "wide", 0)
-    row_count = segment.shape[0]
-    block_rows = math.gcd(row_count, 512)
-
-    def one_block(element):
-        part_rows, part_tags = element
-        running = slot_scan(
-            empty_state(block_rows, head_count),
-            enc_kv,
-            first_slot,
-            part_rows.reshape(block_rows, head_count, HEAD_DIM),
-            part_tags,
-        )
-        return finish(running)
-
-    blocks_out = lax.map(
-        one_block,
-        (
-            segment.reshape(row_count // block_rows, block_rows, segment.shape[1]),
-            holder.reshape(row_count // block_rows, block_rows),
-        ),
-    )
-    partial_context = blocks_out.reshape(row_count, segment.shape[1])
-    context = sum_at_owner(partial_context.astype(jnp.bfloat16), "wide", 0).astype(jnp.bfloat16)
-    return layer_tail(
-        context, hidden_in, norm_gain, router_proj, expert_ids, attn_proj, proj_in, proj_out
+        name="layer_step",
+    )(
+        owner_slot,
+        lang_ids.reshape(8, rows_all),
+        hidden_in,
+        norm_gain.reshape(1, -1),
+        router_parts,
+        expert_ids,
+        queries,
+        enc_kv,
+        attn_proj,
+        proj_in,
+        proj_out,
     )
 
 
 def solution(mesh):
     return jax.shard_map(
-        shards,
+        layer_step,
         mesh=mesh,
         in_specs=(
             P(("wide", "narrow"), "depth"),

time: 136 us -> 101 us (0.74)
  Pallas kernels: 63.2 us -> 94.2 us
  waiting for transfers between devices: 29.8 us -> 0 us
  matrix products: 11.6 us -> 0 us
  starting transfers between devices: 11.4 us -> 0 us
  other arithmetic: 9.29 us -> 1.62 us
  local copies, waits for them, and re-layouts: 10.2 us -> 4.41 us
    pallas_call x1, Pallas kernels: 63.2 us -> 94.2 us  [layer_step(): pl.pallas_call(layer_kernel, out_shape=jax.ShapeDtypeStruct((rows, quarte...]
    all_to_all x2 -> x0, waiting for transfers between devices: 29.8 us -> none  [the longest x1 15 us: sent_to_all(): lax.all_to_all(jnp.broadcast_to(value[None], (peers, *value.shape)), axis...]
    dot_general x8 -> x0, matrix products: 11.6 us -> none  [the longest x4 7.1 us: slot_update(): jnp.einsum('rhk,khd->rhd', weights.astype(jnp.bfloat16), value_rows, pref...]
    all_to_all x2 -> x0, starting transfers between devices: 11.4 us -> none  [the longest x1 7.89 us: sent_to_all(): lax.all_to_all(jnp.broadcast_to(value[None], (peers, *value.shape)), axis...]
    reduce_sum x6 -> x0, other arithmetic: 8.3 us -> none  [the longest x4 6.68 us: slot_update(): run_sum = run_sum * shrink + jnp.sum(weights, axis=2)]
    dynamic_update_slice x8 -> x0, local copies, waits for them, and re-layouts: 3.43 us -> none  [shards(): lax.map(one_block, (segment.reshape(row_count // block_rows, block_rows,...]
    broadcast_in_dim x2 -> x1, local copies, waits for them, and re-layouts: 2.01 us -> 0.01 us  [layer_step(): jnp.zeros_like(low)]
    while x1 -> x0, local copies, waits for them, and re-layouts: 1.41 us -> none  [shards(): lax.map(one_block, (segment.reshape(row_count // block_rows, block_rows,...]
  transfers between devices with their start and end apart: 2 -> 0, of which waited for: 2 -> 0; matrix products, arithmetic and copies ran while one was open for 3% -> 0% of each run, Pallas kernels for 0% -> 0%
where the time goes in v2:
time: 101 us; the launch traced here: 100 us
  Pallas kernels  94.2 us (93%)
  local copies, waits for them, and re-layouts  4.41 us (4%)
  other arithmetic  1.62 us (2%)
    pallas_call x1, Pallas kernels, layer_step(): pl.pallas_call(layer_kernel, out_shape=jax.ShapeDtypeStruct((rows, quarte...  94.2 us
    unnamed x2, local copies, waits for them, and re-layouts  3.04 us

profile of v2, /device:TPU:0, one launch (start us, length us, event | category | flops | bytes accessed | tf_op | source)
XLA Modules:
  0.0 100.2 jit_solution(7968791146463503168)
XLA Ops:
  0.0 0.1 pad.3.clone
  0.1 1.3 %reshape.6.lang_rows = s32[8,256]{1,0:T(8,128)} reshape(s32[2048]{0:T(1024)} %param.13) | data formatting | bytes 16384 | tf_op jit(solution)/shard_map/reshape | solution.py:495
  1.4 0.9 reduce-precision_convert_fusion.1
  2.3 0.7 maximum_maximum_fusion.router_parts
  3.0 1.5 %copy.12.expert_ids = s32[256,2]{1,0:T(8,128)} copy(s32[256,2]{0,1:T(2,128)} %param.19) | data formatting | bytes 4096 | tf_op args[8]
  4.5 94.2 %layer_step.1 = bf16[64,1024]{1,0:T(8,128)(2,1)} custom-call(s32[8]{0:T(128)} %owner_slot.1, s32[8,256]{1,0:T(8,128)} %reshape.6.lang_rows, bf16[64,1024]{1,0:T(8,128)(2,1)} %hidden_in.1, f32[1,4096]{1,0:T(1,128)} %bitcast.8, bf16[16,4096]{1,0:T(8,128)(2,1)} %maximum_maximum_fusion.router_parts, s32[256,2]{1,0:T(8,128)} %copy.12.expert_ids, ...), custom_call_target="tpu_custom_call" | custom-call | tf_op jit(solution)/shard_map/layer_step/pallas_call | solution.py:457
  98.7 1.6 %copy.14 = bf16[64,1024]{1,0:T(8,128)(2,1)} copy(bf16[64,1024]{1,0:T(8,128)(2,1)} %layer_step.1) | data formatting | bytes 262144
  (1 shorter events, 0.0 us)

commit v3 on v2

v3 whole, which is shorter than its diff:
```python
import math

import jax
import jax.numpy as jnp
from jax import lax
from jax.experimental import pallas as pl
from jax.experimental.pallas import tpu as pltpu
from jax.sharding import PartitionSpec as P

HEAD_DIM = 64
MESH = pl.DeviceIdType.MESH


norm_eps = 1e-06


def remote(src, dst, sems, slot, target):
    send_sems, recv_sems = sems
    return pltpu.make_async_remote_copy(
        src_ref=src,
        dst_ref=dst,
        send_sem=send_sems.at[slot],
        recv_sem=recv_sems.at[slot],
        device_id=target,
        device_id_type=MESH,
    )


def places():
    y, d = lax.axis_index("narrow"), lax.axis_index("depth")
    x_lo, core = d // 2, d % 2
    return {
        "y": y,
        "d": d,
        "x": x_lo,
        "core": core,
        "up": (y + 1) % 4,
        "down": (y + 3) % 4,
        "far": (y + 2) % 4,
        "mate_d": x_lo * 2 + (1 - core),
        "side_d": (1 - x_lo) * 2 + core,
        "mate_side_d": (1 - x_lo) * 2 + (1 - core),
        "to_mate": {"depth": x_lo * 2 + (1 - core)},
        "to_side": {"depth": (1 - x_lo) * 2 + core},
        "to_up": {"narrow": (y + 1) % 4},
        "to_down": {"narrow": (y + 3) % 4},
    }


def scatter_sum(at, sems, base, part, own, mate_out, mate_in, ring_out, ring_in, side_out, side_in, finish):
    rows_all, quarter = own.shape[1:]
    rows, sub = rows_all // 4, quarter // 2
    pieces = [pl.ds(j * sub, sub) for j in range(2)]

    def bf16(value):
        return value.astype(jnp.bfloat16)

    def f32(value):
        return value.astype(jnp.float32)

    def rows_of(y):
        return pl.ds(pl.multiple_of(y * rows, rows), rows)

    def mate_copy(which, j):
        there = (which, slice(None), pieces[j])
        return remote(mate_out.at[there], mate_in.at[there], sems, base + which * 2 + j, at["to_mate"])

    def ring_copy(slot, j):
        there = (slot, slice(None), pieces[j])
        target = at["to_up"] if slot < 3 else at["to_down"]
        return remote(ring_out.at[there], ring_in.at[there], sems, base + 4 + slot * 2 + j, target)

    def side_copy(j):
        there = (slice(None), pieces[j])
        return remote(side_out.at[there], side_in.at[there], sems, base + 16 + j, at["to_side"])

    def produce(which, j):
        theirs, ours = ("mate_side_d", "side_d") if which else ("mate_d", "d")
        col = pl.multiple_of(at[theirs] * quarter + j * sub, sub)
        mate_out[which, :, pieces[j]] = bf16(part(col, sub))
        mate_copy(which, j).start()
        col = pl.multiple_of(at[ours] * quarter + j * sub, sub)
        own[which, :, pieces[j]] = part(col, sub)

    def pair(which, y, j):
        return own[which, rows_of(y), pieces[j]] + f32(mate_in[which, rows_of(y), pieces[j]])

    def got(slot, j):
        return f32(ring_in[slot, :, pieces[j]])

    def send(slot, j, value):
        ring_out[slot, :, pieces[j]] = bf16(value)
        ring_copy(slot, j).start()

    up, down, far, y = at["up"], at["down"], at["far"], at["y"]
    produce(1, 0)
    produce(1, 1)
    mate_copy(1, 0).wait_recv()
    send(3, 0, pair(1, far, 0))
    send(1, 0, pair(1, up, 0))
    produce(0, 0)
    mate_copy(1, 1).wait_recv()
    send(3, 1, pair(1, far, 1))
    send(1, 1, pair(1, up, 1))
    produce(0, 1)
    for j in range(2):
        mate_copy(0, j).wait_recv()
        send(0, j, pair(0, far, j))
    send(4, 0, pair(0, down, 0))
    for j in range(2):
        ring_copy(3, j).wait_recv()
        send(5, j, pair(1, down, j) + got(3, j))
    send(4, 1, pair(0, down, 1))
    for j in range(2):
        ring_copy(0, j).wait_recv()
        send(2, j, pair(0, up, j) + got(0, j))
    for j in range(2):
        ring_copy(1, j).wait_recv()
        ring_copy(5, j).wait_recv()
        side_out[:, pieces[j]] = bf16(pair(1, y, j) + got(1, j) + got(5, j))
        side_copy(j).start()
    for j in range(2):
        ring_copy(4, j).wait_recv()
        ring_copy(2, j).wait_recv()
        mine = pair(0, y, j) + got(4, j) + got(2, j)
        side_copy(j).wait_recv()
        finish(pieces[j], mine + f32(side_in[:, pieces[j]]))

    def wait_sent():
        for j in range(2):
            for which in range(2):
                mate_copy(which, j).wait_send()
            for slot in range(6):
                ring_copy(slot, j).wait_send()
            side_copy(j).wait_send()

    return wait_sent


def gather_all(at, sems, base, full, ready):
    rows, quarter = full.shape[0] // 4, full.shape[1] // 4
    sub = quarter // 2

    def block(y, d, piece):
        here = pl.ds(pl.multiple_of(y * rows, rows), rows)
        if piece is None:
            return full.at[here, pl.ds(pl.multiple_of(d * quarter, quarter), quarter)]
        return full.at[here, pl.ds(pl.multiple_of(d * quarter + piece * sub, sub), sub)]

    y, d, mate, side, mate_side = at["y"], at["d"], at["mate_d"], at["side_d"], at["mate_side_d"]
    up, down, far = at["up"], at["down"], at["far"]
    sent = []

    def send(slot, y, d, piece, target):
        ref = block(y, d, piece)
        copy = remote(ref, ref, sems, base + slot, at[target])
        copy.start()
        sent.append(copy)

    def arrived(slot, y, d, piece):
        ref = block(y, d, piece)
        remote(ref, ref, sems, base + slot, at["to_mate"]).wait_recv()

    send(0, y, d, 0, "to_side")
    send(2, y, d, 0, "to_up")
    send(4, y, d, 1, "to_down")
    send(1, y, d, 1, "to_side")
    send(3, y, d, 1, "to_up")
    send(5, y, d, 0, "to_down")
    send(6, y, d, None, "to_mate")
    arrived(0, y, side, 0)
    send(7, y, side, 0, "to_up")
    send(8, y, side, 0, "to_down")
    arrived(1, y, side, 1)
    send(9, y, side, 1, "to_down")
    send(10, y, side, 1, "to_up")
    send(11, y, side, None, "to_mate")
    arrived(2, down, d, 0)
    send(12, down, d, 0, "to_up")
    arrived(4, up, d, 1)
    send(13, up, d, 1, "to_down")
    arrived(3, down, d, 1)
    send(14, down, d, None, "to_mate")
    arrived(5, up, d, 0)
    send(15, up, d, None, "to_mate")
    arrived(6, y, mate, None)
    arrived(11, y, mate_side, None)
    ready(y)
    arrived(7, down, side, 0)
    send(16, down, side, 0, "to_up")
    arrived(9, up, side, 1)
    send(17, up, side, 1, "to_down")
    arrived(10, down, side, 1)
    send(18, down, side, None, "to_mate")
    arrived(8, up, side, 0)
    send(19, up, side, None, "to_mate")
    arrived(12, far, d, 0)
    arrived(13, far, d, 1)
    send(20, far, d, None, "to_mate")
    arrived(14, down, mate, None)
    arrived(18, down, mate_side, None)
    ready(down)
    arrived(16, far, side, 0)
    send(21, far, side, 0, "to_mate")
    arrived(17, far, side, 1)
    send(22, far, side, 1, "to_mate")
    arrived(15, up, mate, None)
    arrived(19, up, mate_side, None)
    ready(up)
    arrived(20, far, mate, None)
    arrived(21, far, mate_side, 0)
    arrived(22, far, mate_side, 1)
    ready(far)

    def wait_sent():
        for copy in sent:
            copy.wait_send()

    return wait_sent


def wide_places():
    w = lax.axis_index("wide")
    z, x = w // 2, w % 2
    up, down, far = (z + 1) % 4, (z + 3) % 4, (z + 2) % 4
    other = 1 - x
    order = [z * 2 + x, up * 2 + x, z * 2 + other, far * 2 + x, up * 2 + other, down * 2 + other, far * 2 + other, down * 2 + x]
    return {"w": w, "order": order}


OWN, UP, SIDE, FAR, UP_SIDE, DOWN_SIDE, FAR_SIDE, DOWN = range(8)
BACK = (OWN, DOWN, SIDE, FAR, DOWN_SIDE, UP_SIDE, FAR_SIDE, UP)


def attend(at, sems, base, set_up, asked, keys, values, marks, answer, returned, context):
    rows, feats = context.shape
    heads = feats // HEAD_DIM
    length = keys.shape[2]
    half = rows // 2
    order = at["order"]

    def send(slot, src_slot, dst_slot, target_slot, part=None):
        src, dst = asked.at[src_slot], asked.at[dst_slot]
        if part is not None:
            here = pl.ds(part * half, half)
            src, dst = asked.at[src_slot, here], asked.at[dst_slot, here]
        remote(src, dst, sems, base + slot, {"wide": order[target_slot]}).start()

    def arrived(slot, dst_slot, part=None):
        dst = asked.at[dst_slot] if part is None else asked.at[dst_slot, pl.ds(part * half, half)]
        remote(dst, dst, sems, base + slot, {"wide": order[SIDE]}).wait_recv()

    send(0, OWN, SIDE, SIDE)
    send(1, OWN, DOWN, UP)
    send(2, OWN, UP, DOWN)

    set_up()
    scale = HEAD_DIM ** (-0.5) * math.log2(math.e)

    def one_block(k, _):
        @pl.when(k == UP)
        def _():
            arrived(1, DOWN)
            send(3, DOWN, FAR, UP, 0)
            arrived(2, UP)
            send(4, UP, FAR, DOWN, 1)
            arrived(0, SIDE)
            send(5, SIDE, DOWN_SIDE, UP)
            send(6, SIDE, UP_SIDE, DOWN)

        @pl.when(k == FAR)
        def _():
            arrived(3, FAR, 0)
            arrived(4, FAR, 1)

        @pl.when(k == UP_SIDE)
        def _():
            arrived(5, DOWN_SIDE)
            send(7, DOWN_SIDE, FAR_SIDE, UP, 0)
            arrived(6, UP_SIDE)
            send(8, UP_SIDE, FAR_SIDE, DOWN, 1)

        @pl.when(k == FAR_SIDE)
        def _():
            arrived(7, FAR_SIDE, 0)
            arrived(8, FAR_SIDE, 1)

        source = jnp.int32(0)
        for slot in range(8):
            source = source + jnp.where(k == slot, order[slot], 0)
        lane = lax.broadcasted_iota(jnp.int32, marks.shape, 1)
        here = jnp.sum(jnp.where(lane == source, marks[...], 0.0), axis=1, keepdims=True)
        query = asked[k]
        total = jnp.zeros((rows, feats), jnp.float32)
        for head in range(heads):
            scores = jnp.dot(query, keys[head], preferred_element_type=jnp.float32)
            top = jnp.max(scores, axis=1, keepdims=True)
            weights = jnp.exp2((scores - top) * scale)
            below = jnp.sum(weights, axis=1, keepdims=True)
            taken = jnp.dot(weights.astype(jnp.bfloat16), values[head], preferred_element_type=jnp.float32)
            total = total + taken * (here / below)
        answer[k] = total.astype(jnp.bfloat16)
        for slot in range(1, 8):

            @pl.when(k == slot)
            def _():
                remote(
                    answer.at[slot], returned.at[BACK[slot]], sems, base + 8 + slot, {"wide": order[slot]}
                ).start()

        return 0

    lax.fori_loop(0, 8, one_block, 0)
    summed = answer[OWN].astype(jnp.float32)
    for slot in range(1, 8):
        remote(answer.at[slot], returned.at[BACK[slot]], sems, base + 8 + slot, {"wide": order[slot]}).wait_recv()
    for slot in range(1, 8):
        summed = summed + returned[slot].astype(jnp.float32)
    context[...] = summed.astype(jnp.bfloat16)

    def wait_sent():
        for slot in range(9):
            part = slot in (3, 4, 7, 8)
            src = asked.at[OWN, pl.ds(0, half)] if part else asked.at[OWN]
            remote(src, src, sems, base + slot, {"wide": order[SIDE]}).wait_send()
        for slot in range(1, 8):
            remote(answer.at[slot], returned.at[BACK[slot]], sems, base + 8 + slot, {"wide": order[slot]}).wait_send()

    return wait_sent


def spread_heads(kv, keys, values):
    heads = keys.shape[0]
    flipped = kv[0].T
    plain = kv[1]
    for head in range(heads):
        place = lax.broadcasted_iota(jnp.int32, flipped.shape, 0) // HEAD_DIM
        keys[head] = jnp.where(place == head, flipped, jnp.zeros_like(flipped))
        place = lax.broadcasted_iota(jnp.int32, plain.shape, 1) // HEAD_DIM
        values[head] = jnp.where(place == head, plain, jnp.zeros_like(plain))


def lay_out_small(router_rows, router_parts, expert_ids, pair_ids):
    exact = router_rows[...]
    high = exact.astype(jnp.bfloat16)
    middle = (exact - high.astype(jnp.float32)).astype(jnp.bfloat16)
    low = (exact - high.astype(jnp.float32) - middle.astype(jnp.float32)).astype(jnp.bfloat16)
    router_parts[...] = jnp.concatenate([high, middle, low, jnp.zeros_like(low)], axis=0)
    pad = jnp.zeros((6, expert_ids.shape[1]), jnp.float32)
    wide_ids = jnp.concatenate([expert_ids[...].astype(jnp.float32), pad], axis=0)
    pair_ids[...] = wide_ids.T.astype(jnp.int32)


def mark_rows(at, lang_ids, owner_slot, marks):
    rows = marks.shape[0]
    group = jnp.int32(0)
    for g in range(owner_slot.shape[0]):
        group = group + jnp.where(owner_slot[g] == at["w"], g, 0)
    spans = [lang_ids[:, block * rows : (block + 1) * rows] for block in range(8)]
    marks[...] = jnp.where(jnp.concatenate(spans, axis=0) == group, 1.0, 0.0).T


def layer_kernel(
    hidden_in_hbm,
    queries_hbm,
    lang_ids_hbm,
    owner_slot_hbm,
    enc_kv_hbm,
    attn_proj_hbm,
    norm_gain_hbm,
    router_rows_hbm,
    expert_ids_hbm,
    proj_in_hbm,
    proj_out_hbm,
    out,
    hidden_in,
    lang_ids,
    owner_slot,
    norm_gain,
    router_rows,
    expert_ids,
    asked,
    kv,
    keys,
    values,
    marks,
    answer,
    returned,
    context,
    attn_proj,
    proj_in,
    proj_out,
    full,
    normed,
    act,
    gate,
    router_parts,
    pair_ids,
    own,
    mate_out,
    mate_in,
    ring_out,
    ring_in,
    side_out,
    side_in,
    load_sems,
    send_sems,
    recv_sems,
):
    at, wide_at = places(), wide_places()
    sems = (send_sems, recv_sems)
    moves = [
        (queries_hbm, asked.at[OWN]),
        (enc_kv_hbm.at[0], kv),
        (lang_ids_hbm, lang_ids),
        (owner_slot_hbm, owner_slot),
        (attn_proj_hbm, attn_proj),
        (hidden_in_hbm, hidden_in),
        (norm_gain_hbm, norm_gain),
        (router_rows_hbm, router_rows),
        (expert_ids_hbm, expert_ids),
        (proj_in_hbm.at[0], proj_in),
        (proj_out_hbm.at[0], proj_out),
    ]
    loads = [pltpu.make_async_copy(src, dst, load_sems.at[i]) for i, (src, dst) in enumerate(moves)]
    loads[0].start()
    barrier = pltpu.get_barrier_semaphore()
    for slot in range(7, 0, -1):
        peer = {"wide": wide_at["order"][slot]}
        pl.semaphore_signal(barrier, inc=1, device_id=peer, device_id_type=MESH)
    for peer in ("to_mate", "to_side", "to_up", "to_down"):
        pl.semaphore_signal(barrier, inc=1, device_id=at[peer], device_id_type=MESH)
    for load in loads[1:]:
        load.start()
    loads[0].wait()
    pl.semaphore_wait(barrier, 11)

    def set_up():
        for i in (1, 2, 3):
            loads[i].wait()
        spread_heads(kv, keys, values)
        mark_rows(wide_at, lang_ids, owner_slot, marks)

    attend_sent = attend(
        wide_at, sems, 0, set_up, asked, keys, values, marks, answer, returned, context
    )
    for i in (4, 5, 6, 7, 8):
        loads[i].wait()

    rows, quarter = hidden_in.shape
    my_rows = pl.ds(pl.multiple_of(at["y"] * rows, rows), rows)

    def my_cols(piece):
        return pl.ds(pl.multiple_of(at["d"] * quarter + piece.start, piece.size), piece.size)

    def proj_part(col, size):
        return jnp.dot(
            context[...], attn_proj[:, pl.ds(col, size)], preferred_element_type=jnp.float32
        )

    def add_residual(piece, value):
        residual = hidden_in[:, piece].astype(jnp.float32) + value
        full[my_rows, my_cols(piece)] = residual.astype(jnp.bfloat16)

    proj_sent = scatter_sum(
        at, sems, 16, proj_part, own, mate_out.at[0], mate_in.at[0], ring_out.at[0], ring_in.at[0],
        side_out.at[0], side_in.at[0], add_residual,
    )
    lay_out_small(router_rows, router_parts, expert_ids, pair_ids)
    strip = 16

    def ready(y):
        def normalise(s, _):
            here = pl.ds(pl.multiple_of(y * rows + s * strip, strip), strip)
            value = full[here, :].astype(jnp.float32)
            inv = lax.rsqrt(jnp.mean(value * value, axis=1, keepdims=True) + norm_eps)
            normed[here, :] = (value * inv * norm_gain[...]).astype(jnp.bfloat16)
            return 0

        lax.fori_loop(0, rows // strip, normalise, 0)
        here = pl.ds(pl.multiple_of(y * rows, rows), rows)
        logit_parts = lax.dot_general(
            normed[here, :], router_parts[...], (((1,), (1,)), ((), ())), preferred_element_type=jnp.float32
        )
        first, second = pair_ids[here, 0:1], pair_ids[here, 1:2]
        chosen = (first == at["y"]) | (second == at["y"])
        other = first + second - at["y"]
        expert_of = lax.broadcasted_iota(jnp.int32, logit_parts.shape, 1) % 4
        signed = jnp.where(expert_of == at["y"], logit_parts, 0.0) - jnp.where(
            expert_of == other, logit_parts, 0.0
        )
        margin = jnp.sum(signed, axis=1, keepdims=True)
        gate[here, :] = jnp.where(chosen, 1.0 / (1.0 + jnp.exp(-margin)), 0.0)

    gather_sent = gather_all(at, sems, 34, full, ready)
    loads[9].wait()
    hidden = act.shape[1]
    step = 256 if hidden % 256 == 0 else hidden

    def first_layer(t, _):
        here = pl.ds(pl.multiple_of(t * step, step), step)
        value = jnp.dot(normed[...], proj_in[:, here], preferred_element_type=jnp.float32)
        act[:, here] = jax.nn.gelu(value, approximate=True).astype(jnp.bfloat16)
        return 0

    lax.fori_loop(0, hidden // step, first_layer, 0)
    loads[10].wait()

    def expert_part(col, size):
        return gate[...] * jnp.dot(
            act[...], proj_out[:, pl.ds(col, size)], preferred_element_type=jnp.float32
        )

    def add_experts(piece, value):
        residual = full[my_rows, my_cols(piece)].astype(jnp.float32)
        out[:, piece] = (residual + value).astype(jnp.bfloat16)

    expert_sent = scatter_sum(
        at, sems, 57, expert_part, own, mate_out.at[1], mate_in.at[1], ring_out.at[1], ring_in.at[1],
        side_out.at[1], side_in.at[1], add_experts,
    )
    for wait_sent in (attend_sent, proj_sent, gather_sent, expert_sent):
        wait_sent()


def layer_step(
    hidden_in,
    queries,
    lang_ids,
    owner_slot,
    enc_kv,
    attn_proj,
    norm_gain,
    router_proj,
    expert_ids,
    proj_in,
    proj_out,
):
    rows_all, inner = queries.shape
    rows, quarter = hidden_in.shape
    width = attn_proj.shape[1]
    hidden = proj_in.shape[2]
    length = enc_kv.shape[2]
    heads = inner // HEAD_DIM
    bf16, f32, i32 = jnp.bfloat16, jnp.float32, jnp.int32
    copies = 75
    return pl.pallas_call(
        layer_kernel,
        out_shape=pltpu.VMEM((rows, quarter), bf16),
        in_specs=[pl.BlockSpec(memory_space=pl.ANY)] * 11,
        out_specs=pl.BlockSpec(memory_space=pltpu.VMEM),
        scratch_shapes=[
            pltpu.VMEM((rows, quarter), bf16),
            pltpu.VMEM((1, lang_ids.shape[0]), i32),
            pltpu.SMEM(owner_slot.shape, i32),
            pltpu.VMEM((1, width), f32),
            pltpu.VMEM((4, width), f32),
            pltpu.VMEM((2, rows_all), i32),
            pltpu.VMEM((8, rows_all, inner), bf16),
            pltpu.VMEM((2, length, inner), bf16),
            pltpu.VMEM((heads, inner, length), bf16),
            pltpu.VMEM((heads, length, inner), bf16),
            pltpu.VMEM((rows_all, 8), f32),
            pltpu.VMEM((8, rows_all, inner), bf16),
            pltpu.VMEM((8, rows_all, inner), bf16),
            pltpu.VMEM((rows_all, inner), bf16),
            pltpu.VMEM((inner, width), bf16),
            pltpu.VMEM((width, hidden), bf16),
            pltpu.VMEM((hidden, width), bf16),
            pltpu.VMEM((rows_all, width), bf16),
            pltpu.VMEM((rows_all, width), bf16),
            pltpu.VMEM((rows_all, hidden), bf16),
            pltpu.VMEM((rows_all, 1), f32),
            pltpu.VMEM((16, width), bf16),
            pltpu.VMEM((rows_all, 8), i32),
            pltpu.VMEM((2, rows_all, quarter), f32),
            pltpu.VMEM((2, 2, rows_all, quarter), bf16),
            pltpu.VMEM((2, 2, rows_all, quarter), bf16),
            pltpu.VMEM((2, 6, rows, quarter), bf16),
            pltpu.VMEM((2, 6, rows, quarter), bf16),
            pltpu.VMEM((2, rows, quarter), bf16),
            pltpu.VMEM((2, rows, quarter), bf16),
            pltpu.SemaphoreType.DMA((11,)),
            pltpu.SemaphoreType.DMA((copies,)),
            pltpu.SemaphoreType.DMA((copies,)),
        ],
        compiler_params=pltpu.CompilerParams(
            collective_id=0, has_side_effects=True, vmem_limit_bytes=60 * 1024 * 1024
        ),
        name="layer_step",
    )(
        hidden_in,
        queries,
        lang_ids.reshape(1, -1),
        owner_slot,
        enc_kv,
        attn_proj,
        norm_gain.reshape(1, -1),
        router_proj.T,
        expert_ids.T,
        proj_in,
        proj_out,
    )


def solution(mesh):
    return jax.shard_map(
        layer_step,
        mesh=mesh,
        in_specs=(
            P(("wide", "narrow"), "depth"),
            P("wide", ("narrow", "depth")),
            P(),
            P(),
            P("wide", None, None, ("narrow", "depth")),
            P(("narrow", "depth"), None),
            P(),
            P(),
            P("wide", None),
            P("narrow", None, "depth"),
            P("narrow", "depth", None),
        ),
        out_specs=P(("wide", "narrow"), "depth"),
        check_vma=False,
    )
```

time: 101 us -> 85.1 us (0.84)
  Pallas kernels: 94.2 us -> 84.4 us
  local copies, waits for them, and re-layouts: 4.41 us -> 0.66 us
  other arithmetic: 1.62 us -> 0 us
    pallas_call x1, Pallas kernels: 94.2 us -> 84.4 us  [layer_step(): pl.pallas_call(layer_kernel, out_shape=pltpu.VMEM((rows, quarter), bf16),...]
    unnamed x2 -> x1, local copies, waits for them, and re-layouts: 3.04 us -> 0.66 us
    reshape x1 -> x0, local copies, waits for them, and re-layouts: 1.29 us -> none  [layer_step(): lang_ids.reshape(8, rows_all)]
where the time goes in v3:
time: 85.1 us; the launch traced here: 85 us
  Pallas kernels  84.4 us (99%)
    pallas_call x1, Pallas kernels, layer_step(): pl.pallas_call(layer_kernel, out_shape=pltpu.VMEM((rows, quarter), bf16),...  84.4 us

profile of v3, /device:TPU:0, one launch (start us, length us, event | category | flops | bytes accessed | tf_op | source)
XLA Modules:
  0.0 85.0 jit_solution(10992767418243051038)
XLA Ops:
  0.0 84.4 %layer_step.1 = bf16[64,1024]{1,0:T(8,128)(2,1)S(1)} custom-call(bf16[64,1024]{1,0:T(8,128)(2,1)} %hidden_in_hbm.1, bf16[256,256]{1,0:T(8,128)(2,1)} %queries_hbm.1, s32[1,2048]{1,0:T(1,128)} %bitcast.6, s32[8]{0:T(128)} %owner_slot_hbm.1, bf16[1,2,768,256]{3,2,1,0:T(8,128)(2,1)} %enc_kv_hbm.1, bf16[256,4096]{1,0:T(8,128)(2,1)} %attn_proj_hbm.1, ...), custom_call_target="tpu_custom_call" | custom-call | tf_op jit(solution)/shard_map/layer_step/pallas_call | solution.py:547
  84.4 0.7 copy.13
